TPU v7x, 256 devices: a whole 4x4x8 slice. The times are simulated.
256 devices in a mesh: section: 8 (over y, z_hi), mp: 32 (over x, z_lo, core).
Axes of the slice: x: 4, y: 4, z: 8 (z_hi: 2, z_lo: 4; z = z_hi * 4 + z_lo), core: 2. Of those that a mesh axis runs over, the one named last changes fastest.
Arguments:
- stream: bfloat16 [4096, 4096], P(('section', 'mp')), may hold values from -6 to 6
- ffn_gain: float32 [4096], replicated, may hold values from 0.25 to 1.75
- router_weight: bfloat16 [4096, 8], replicated, may hold values from -0.1875 to 0.1875
- expert_ids: int32 [4096, 2], P(('section', 'mp')), may hold values from 0 to 7, all different within a row; in each aligned block of 16 rows (0 to 15, 16 to 31, ...) at most 6 rows name the same one
- w_gate: bfloat16 [8, 4096, 14336], P('section', None, 'mp'), may hold values from -0.09375 to 0.09375
- w_up: bfloat16 [8, 4096, 14336], P('section', None, 'mp'), may hold values from -0.09375 to 0.09375
- w_down: bfloat16 [8, 14336, 4096], P('section', 'mp'), may hold values from -0.09375 to 0.09375
- attn_gain: float32 [4096], replicated, may hold values from 0.25 to 1.75
- w_kv: bfloat16 [4096, 2048], P(None, 'mp'), may hold values from -0.09375 to 0.09375
Outputs:
- stream_out: bfloat16 [4096, 4096], P(('section', 'mp'))
- kv_decode: bfloat16 [4096, 2048], P('section', 'mp')
Inputs may be any that keep to these rules, and one draw needn't show every extreme that they name: `expert_ids`: each row names two different experts. Among the rows of one device no expert is named more than 6 times, a bound that some block reaches.
All inputs are finite; a program needn't handle non-finite values.
Results may differ from a plain program's by a relative error of at most 0.02.
Values may be sent and summed in bfloat16 or wider, within the bound.
A program may use at most 128 MiB of HBM per device.

v0:
```python
import jax
import jax.numpy as jnp
from jax import lax
from jax.sharding import PartitionSpec as P

epsilon = 1e-05


def shifted(value, axis, steps):
    count = lax.axis_size(axis)
    pairs = [(source, (source + steps) % count) for source in range(count)]
    return lax.ppermute(value, axis, pairs)


def normalize(values, scale_gain):
    floats = values.astype(jnp.float32)
    return (
        floats * lax.rsqrt(jnp.mean(floats * floats, axis=-1, keepdims=True) + epsilon) * scale_gain
    )


def body(stream, ffn_gain, router_weight, expert_ids, w_gate, w_up, w_down, attn_gain, w_kv):
    own_rows = stream.shape[0]
    model_width = stream.shape[1]
    experts = router_weight.shape[1]
    capacity = min(own_rows, 3 * own_rows // experts)
    normed = normalize(stream, ffn_gain).astype(jnp.bfloat16)
    logits = jnp.dot(normed, router_weight, preferred_element_type=jnp.float32)
    onehot = expert_ids[:, :, None] == jnp.arange(experts, dtype=jnp.int32)[None, None, :]
    chosen = jnp.sum(jnp.where(onehot, logits[:, None, :], jnp.float32(0.0)), axis=-1)
    share_first = jax.nn.sigmoid(chosen[:, 0] - chosen[:, 1])
    flat_hits = onehot.reshape(own_rows * 2, experts).astype(jnp.int32)
    before = jnp.cumsum(flat_hits, axis=0) - flat_hits
    slot_index = jnp.sum(before * flat_hits, axis=-1)
    expert_flat = expert_ids.reshape(-1)
    route_table = (
        expert_flat[None, None, :] == jnp.arange(experts, dtype=jnp.int32)[:, None, None]
    ) & (slot_index[None, None, :] == jnp.arange(capacity, dtype=jnp.int32)[None, :, None])
    route_table = route_table.astype(jnp.bfloat16)
    repeated = jnp.repeat(normed, 2, axis=0)
    buffer = jnp.einsum(
        "ecr,rd->ecd", route_table, repeated, preferred_element_type=jnp.float32
    ).astype(jnp.bfloat16)
    arrived = lax.all_to_all(buffer, "section", split_axis=0, concat_axis=0, tiled=True)
    inbound = arrived.reshape(experts * capacity, model_width)
    gate_weight = w_gate[0]
    up_weight = w_up[0]
    down_weight = w_down[0]
    block_rows = lax.all_gather(inbound, "mp", axis=0, tiled=True)
    gate_part = jnp.dot(block_rows, gate_weight, preferred_element_type=jnp.float32)
    up_part = jnp.dot(block_rows, up_weight, preferred_element_type=jnp.float32)
    hidden_all = (jax.nn.silu(gate_part) * up_part).astype(jnp.bfloat16)
    block_rows = hidden_all
    summed = lax.psum_scatter(
        jnp.dot(block_rows, down_weight, preferred_element_type=jnp.float32).astype(jnp.bfloat16),
        "mp",
        scatter_dimension=0,
        tiled=True,
    )
    results = summed.reshape(experts, capacity, model_width)
    returned = lax.all_to_all(results, "section", split_axis=0, concat_axis=0, tiled=True)
    picked = jnp.einsum("ecr,ecd->rd", route_table, returned, preferred_element_type=jnp.float32)
    picked = picked.reshape(own_rows, 2, model_width)
    updated = (
        stream.astype(jnp.float32)
        + share_first[:, None] * picked[:, 0]
        + (1.0 - share_first)[:, None] * picked[:, 1]
    )
    stream_out = updated.astype(jnp.bfloat16)
    attn_input = normalize(stream_out, attn_gain).astype(jnp.bfloat16)
    kv_local = jnp.dot(
        lax.all_gather(attn_input, "mp", axis=0, tiled=True),
        w_kv,
        preferred_element_type=jnp.float32,
    ).astype(jnp.bfloat16)
    kv_decode = shifted(kv_local, "section", 1)
    return (stream_out, kv_decode)


def solution(mesh):
    in_specs = (
        P(("section", "mp"), None),
        P(),
        P(),
        P(("section", "mp"), None),
        P("section", None, "mp"),
        P("section", None, "mp"),
        P("section", "mp", None),
        P(),
        P(None, "mp"),
    )
    out_specs = (P(("section", "mp"), None), P("section", "mp"))
    return jax.shard_map(body, mesh=mesh, in_specs=in_specs, out_specs=out_specs, check_vma=False)
```

profile of v0, /device:TPU:3, one launch (start us, length us, event | category | flops | bytes accessed | tf_op | source)
XLA Modules:
  0.0 427.5 jit_solution(1676911125095666726)
XLA Ops:
  7.2 0.8 copy.31
  8.0 0.1 eq.61
  8.1 0.1 fusion.29
  8.2 1.1 fusion.20
  9.3 0.1 reduce_window_sum.11
  9.3 0.2 select_reduce_fusion
  9.5 1.0 fusion.22
  10.5 0.2 broadcast_in_dim.16
  10.7 0.1 reshape.91
  10.8 0.2 convolution_convert_fusion.1
  11.1 0.2 copy.32
  11.3 24.8 %all_to_all.10 = bf16[8,6,4096]{2,1,0:T(8,128)(2,1)S(1)} all-to-all(bf16[8,6,4096]{2,1,0:T(8,128)(2,1)S(1)} %copy.32), channel_id=1, replica_groups=mesh['section'=8,'mp'=32] {'section'}, dimensions={0} | all-to-all | bytes 786432 | tf_op jit(solution)/shard_map/all_to_all | solution.py:44
  36.1 0.9 reshape.88
  37.1 80.0 %all-gather.3.cloned.1.call-done = bf16[1536,4096]{1,0:T(8,128)(2,1)} async-done(((bf16[48,4096]{1,0:T(8,128)(2,1)}), bf16[1536,4096]{1,0:T(8,128)(2,1)}) %all-gather.3.cloned.1.call-update) | async-done | bytes 12582928 | tf_op jit(solution)/shard_map/all_gather | solution.py:49
  117.1 9.7 %fusion.3 = f32[1536,448]{0,1:T(8,128)S(1)} fusion(bf16[1536,4096]{1,0:T(8,128)(2,1)} %all-gather.3.cloned.1.call-done, bf16[1,4096,448]{1,2,0:T(8,128)(2,1)} %param.13), kind=kOutput, calls=%fused_computation.6 | convolution fusion | flops 5637144576 | bytes 19005440 | tf_op jit(solution)/shard_map/dot_general | solution.py:50
  126.8 24.2 %convolution_convert_fusion = bf16[1536,4096]{1,0:T(8,128)(2,1)} fusion(bf16[1,448,4096]{2,1,0:T(8,128)(2,1)} %param.15, bf16[1536,4096]{1,0:T(8,128)(2,1)} %all-gather.3.cloned.1.call-done, bf16[1,4096,448]{1,2,0:T(8,128)(2,1)} %param.14, f32[1536,448]{0,1:T(8,128)S(1)} %fusion.3), kind=kOutput, calls=%fused_computation | convolution fusion | flops 11284709376 | bytes 35258368 | tf_op jit(solution)/shard_map/dot_general | solution.py:55
  151.0 154.0 %reduce-scatter.2.cloned.1.call-done = bf16[48,4096]{1,0:T(8,128)(2,1)} async-done(((bf16[1536,4096]{1,0:T(8,128)(2,1)}), bf16[48,4096]{1,0:T(8,128)(2,1)}) %reduce-scatter.2.cloned.1.call-update) | async-done | bytes 393232 | tf_op jit(solution)/shard_map/reduce_scatter | solution.py:54
  305.0 1.9 reshape.89
  306.9 8.1 %all-to-all-start.1 = ((bf16[8,6,4096]{2,1,0:T(8,128)(2,1)}), bf16[8,6,4096]{2,1,0:T(8,128)(2,1)S(1)}, u32[]{:S(2)}, u32[]{:S(2)}) async-start(bf16[8,6,4096]{2,1,0:T(8,128)(2,1)} %reshape.89), calls=%async_computation.2 | async-start | bytes 1048576 | tf_op jit(solution)/shard_map/all_to_all | solution.py:61
  315.1 0.2 all-gather.5.cloned.1.call-start
  315.3 0.2 fusion.37
  315.5 12.2 %all-to-all-done.1 = bf16[8,6,4096]{2,1,0:T(8,128)(2,1)S(1)} async-done(((bf16[8,6,4096]{2,1,0:T(8,128)(2,1)}), bf16[8,6,4096]{2,1,0:T(8,128)(2,1)S(1)}, u32[]{:S(2)}, u32[]{:S(2)}) %all-to-all-start.1) | async-done | bytes 393248 | tf_op jit(solution)/shard_map/all_to_all | solution.py:61
  327.6 0.3 convolution_bitcast_fusion
  328.0 0.3 reshape.90
  328.3 0.5 fusion.36
  328.9 0.4 fusion.17
  329.3 0.7 fusion.19
  330.1 77.3 %all-gather.5.cloned.1.call-done = bf16[512,4096]{1,0:T(8,128)(2,1)} async-done(((bf16[16,4096]{1,0:T(8,128)(2,1)}), bf16[512,4096]{1,0:T(8,128)(2,1)}) %all-gather.5.cloned.1.call-update) | async-done | bytes 4194320 | tf_op jit(solution)/shard_map/all_gather | solution.py:72
  407.4 3.6 convolution_convert_fusion.2
  411.0 3.7 collective-permute-start
  414.7 5.6 %collective-permute-done = bf16[512,64]{0,1:T(8,128)(2,1)S(1)} collective-permute-done((bf16[512,64]{0,1:T(8,128)(2,1)S(1)}, bf16[512,64]{0,1:T(8,128)(2,1)S(1)}, u32[]{:S(2)}, u32[]{:S(2)}) %collective-permute-start) | collective-permute-done | bytes 65568 | tf_op jit(solution)/shard_map/ppermute | solution.py:12
  420.3 0.6 copy.53
  (23 shorter events, 0.2 us)
Async XLA Ops:
  7.2 400.2 %copy-start = (bf16[4096,64]{0,1:T(8,128)(2,1)S(1)}, bf16[4096,64]{0,1:T(8,128)(2,1)}, u32[]{:S(2)}) copy-start(bf16[4096,64]{0,1:T(8,128)(2,1)} %param.17) | copy-start | bytes 1572868
  7.2 109.9 %all-gather.3.cloned.1.call-start = ((), (), s32[]{:S(2)}) async-start(), calls=%async_computation.3 | async-start | bytes 12976128 | tf_op jit(solution)/shard_map/all_gather | solution.py:49
  37.0 268.0 %reduce-scatter.2.cloned.1.call-start = ((), (), s32[]{:S(2)}) async-start(), calls=%async_computation.4 | async-start | bytes 12976128 | tf_op jit(solution)/shard_map/reduce_scatter | solution.py:54
  151.0 164.3 %copy-start.3 = (bf16[4096,8]{0,1:T(8,128)(2,1)S(1)}, bf16[4096,8]{0,1:T(8,128)(2,1)}, u32[]{:S(2)}) copy-start(bf16[4096,8]{0,1:T(8,128)(2,1)} %param.11) | copy-start | bytes 196612
  151.0 164.5 %copy-start.5 = (s32[16,2]{0,1:T(2,128)S(1)}, s32[16,2]{0,1:T(2,128)}, u32[]{:S(2)}) copy-start(s32[16,2]{0,1:T(2,128)} %param.12) | copy-start | bytes 388
  151.0 177.9 %copy-start.1 = (bf16[16,4096]{1,0:T(8,128)(2,1)S(1)}, bf16[16,4096]{1,0:T(8,128)(2,1)}, u32[]{:S(2)}) copy-start(bf16[16,4096]{1,0:T(8,128)(2,1)} %param.9) | copy-start | bytes 393220
  151.0 178.3 %copy-start.4 = (f32[4096]{0:T(1024)S(1)}, f32[4096]{0:T(1024)}, u32[]{:S(2)}) copy-start(f32[4096]{0:T(1024)} %param.16) | copy-start | bytes 49156
  306.9 20.7 %all-to-all-start.1 = ((bf16[8,6,4096]{2,1,0:T(8,128)(2,1)}), bf16[8,6,4096]{2,1,0:T(8,128)(2,1)S(1)}, u32[]{:S(2)}, u32[]{:S(2)}) async-start(bf16[8,6,4096]{2,1,0:T(8,128)(2,1)} %reshape.89), calls=%async_computation.2 | async-start | bytes 1048576 | tf_op jit(solution)/shard_map/all_to_all | solution.py:61
  315.1 92.3 %all-gather.5.cloned.1.call-start = ((), (), s32[]{:S(2)}) async-start(), calls=%async_computation.5 | async-start | bytes 4325376 | tf_op jit(solution)/shard_map/all_gather | solution.py:72
  329.3 91.6 %copy-start.2 = (bf16[16,4096]{1,0:T(8,128)(2,1)}, bf16[16,4096]{1,0:T(8,128)(2,1)S(1)}, u32[]{:S(2)}) copy-start(bf16[16,4096]{1,0:T(8,128)(2,1)S(1)} %get-tuple-element.10) | copy-start | bytes 393220
  411.0 9.3 %collective-permute-start = (bf16[512,64]{0,1:T(8,128)(2,1)S(1)}, bf16[512,64]{0,1:T(8,128)(2,1)S(1)}, u32[]{:S(2)}, u32[]{:S(2)}) collective-permute-start(bf16[512,64]{0,1:T(8,128)(2,1)S(1)} %convolution_convert_fusion.2), channel_id=1, source_target_pairs={{0,32},{32,64},{64,96},{96,128},{128,160},{160,192},{192,224},{224... | collective-permute-start | bytes 196616 | tf_op jit(solution)/shard_map/ppermute | solution.py:12
Sparse Core Ops, SparseCore 0:
  37.1 79.8 all-gather.2
  151.1 153.8 reduce-scatter.1
  330.2 77.1 all-gather.4
where the time goes:
time: 429 us; the launch traced here: 427 us
  waiting for transfers between devices  329 us (77%)
  matrix products  38.2 us (9%)
  blocking collectives  24.8 us (6%)
  between operations  13.9 us (3%)
  starting transfers between devices  12.1 us (3%)
  local copies, waits for them, and re-layouts  5.75 us (1%)
    reduce_scatter x1, waiting for transfers between devices, body(): lax.psum_scatter(jnp.dot(block_rows, down_weight, preferred_element_type=...  154 us
    all_gather x1, waiting for transfers between devices, body(): block_rows = lax.all_gather(inbound, 'mp', axis=0, tiled=True)  80 us
    all_gather x1, waiting for transfers between devices, body(): lax.all_gather(attn_input, 'mp', axis=0, tiled=True)  77.3 us
    all_to_all x1, blocking collectives, body(): lax.all_to_all(buffer, 'section', split_axis=0, concat_axis=0, tiled=True)  24.8 us
    dot_general x1, matrix products, body(): jnp.dot(block_rows, down_weight, preferred_element_type=jnp.float32)  24.2 us
    all_to_all x1, waiting for transfers between devices, body(): lax.all_to_all(results, 'section', split_axis=0, concat_axis=0, tiled=True)  12.2 us
    dot_general x1, matrix products, body(): jnp.dot(block_rows, gate_weight, preferred_element_type=jnp.float32)  9.7 us
  transfers between devices with their start and end apart: 5, of which 5 were waited for; matrix products, arithmetic and copies ran while one was open for 0% of the time, Pallas kernels for 0%

commit v1 on v0

--- a/solution.py
+++ b/solution.py
@@ -1,15 +1,17 @@
+import functools
+
 import jax
 import jax.numpy as jnp
 from jax import lax
+from jax.experimental import pallas as pl
+from jax.experimental.pallas import tpu as pltpu
 from jax.sharding import PartitionSpec as P
 
 epsilon = 1e-05
-
-
-def shifted(value, axis, steps):
-    count = lax.axis_size(axis)
-    pairs = [(source, (source + steps) % count) for source in range(count)]
-    return lax.ppermute(value, axis, pairs)
+MESH = pl.DeviceIdType.MESH
+NX = 4
+NZ = 4
+VMEM_LIMIT = 66_000_000
 
 
 def normalize(values, scale_gain):
@@ -17,6 +19,422 @@
     return (
         floats * lax.rsqrt(jnp.mean(floats * floats, axis=-1, keepdims=True) + epsilon) * scale_gain
     )
+
+
+class Place:
+    def __init__(self):
+        self.s = lax.axis_index("section")
+        m = lax.axis_index("mp")
+        self.x = m // (NZ * 2)
+        self.z = (m // 2) % NZ
+        self.c = m % 2
+        z = self.z
+        self.cols = [self.x, (self.x + 3) % NX, (self.x + 1) % NX, (self.x + 2) % NX]
+        self.zs = [z, z + 1 - 2 * (z % 2), (z + 2) % NZ, NZ - 1 - z]
+
+    def at(self, x, z, c):
+        return (self.s, x * (NZ * 2) + z * 2 + c)
+
+    def partner(self):
+        return self.at(self.x, self.z, 1 - self.c)
+
+    def side(self, way):
+        return self.at(self.cols[2 - way], self.z, self.c)
+
+    def zpeer(self, k):
+        return self.at(self.x, self.zs[k], self.c)
+
+    def peers(self):
+        return [self.partner(), self.side(0), self.side(1)] + [self.zpeer(k) for k in (1, 2, 3)]
+
+
+class Gather:
+    def __init__(self, place, X, sems):
+        self.p, self.X = place, X
+        self.zs_s, self.zs_r, self.xs_s, self.xs_r, self.x2_s, self.x2_r, self.p_s, self.p_r = sems
+        self.half = X.shape[-1] // 2
+
+    @staticmethod
+    def sems():
+        dma = pltpu.SemaphoreType.DMA
+        return [dma((3,)), dma((3,)), dma((2, 4)), dma((2, 4)), dma((2, 4)), dma((2, 4)), dma((4, 4)), dma((4, 4))]
+
+    def block(self, r, q, c):
+        return self.X.at[self.p.cols[r], self.p.zs[q], c]
+
+    def copy(self, ref, send, recv, to):
+        return pltpu.make_async_remote_copy(
+            src_ref=ref, dst_ref=ref, send_sem=send, recv_sem=recv, device_id=to, device_id_type=MESH
+        )
+
+    def to_z(self, k):
+        return self.copy(self.block(0, 0, self.p.c), self.zs_s.at[k - 1], self.zs_r.at[k - 1], self.p.zpeer(k))
+
+    def from_z(self, k):
+        return self.copy(self.block(0, k, self.p.c), self.zs_s.at[k - 1], self.zs_r.at[k - 1], self.p.zpeer(k))
+
+    def to_x(self, way, q):
+        return self.copy(self.block(0, q, self.p.c), self.xs_s.at[way, q], self.xs_r.at[way, q], self.p.side(way))
+
+    def from_x(self, way, q):
+        return self.copy(self.block(1 + way, q, self.p.c), self.xs_s.at[way, q], self.xs_r.at[way, q], self.p.side(way))
+
+    def part(self, r, q, way):
+        return self.X.at[self.p.cols[r], self.p.zs[q], self.p.c, :, pl.ds(way * self.half, self.half)]
+
+    def on_x(self, way, q):
+        return self.copy(self.part(1 + way, q, way), self.x2_s.at[way, q], self.x2_r.at[way, q], self.p.side(way))
+
+    def from_x2(self, way, q):
+        return self.copy(self.part(3, q, way), self.x2_s.at[way, q], self.x2_r.at[way, q], self.p.side(way))
+
+    def pair(self, r, q):
+        return self.copy(self.block(r, q, self.p.c), self.p_s.at[r, q], self.p_r.at[r, q], self.p.partner())
+
+    def from_pair(self, r, q):
+        return self.copy(self.block(r, q, 1 - self.p.c), self.p_s.at[r, q], self.p_r.at[r, q], self.p.partner())
+
+    def start(self):
+        self.to_x(0, 0).start()
+        self.to_x(1, 0).start()
+        for k in (1, 2, 3):
+            self.to_z(k).start()
+        self.pair(0, 0).start()
+
+    def spread_z(self, k):
+        self.from_z(k).wait_recv()
+        self.to_x(0, k).start()
+        self.to_x(1, k).start()
+        self.pair(0, k).start()
+
+    def spread_x(self, q):
+        for way in (0, 1):
+            self.from_x(way, q).wait_recv()
+            self.on_x(way, q).start()
+        for way in (0, 1):
+            self.pair(1 + way, q).start()
+
+    def spread_x2(self, q):
+        for way in (0, 1):
+            self.from_x2(way, q).wait_recv()
+        self.pair(3, q).start()
+
+    def need(self, r, qs):
+        for q in qs:
+            self.from_pair(r, q).wait_recv()
+
+    def finish(self):
+        for k in (1, 2, 3):
+            self.to_z(k).wait_send()
+        for q in range(4):
+            for way in (0, 1):
+                self.to_x(way, q).wait_send()
+                self.on_x(way, q).wait_send()
+            for r in range(4):
+                self.pair(r, q).wait_send()
+
+
+def enter(peers):
+    barrier = pltpu.get_barrier_semaphore()
+    for peer in peers:
+        pl.semaphore_signal(barrier, inc=1, device_id=peer, device_id_type=MESH)
+    pl.semaphore_wait(barrier, len(peers))
+
+
+class Reduce:
+    def __init__(self, place, Y, PR, RX, RH, RZ, sems):
+        self.p, self.Y, self.PR, self.RX, self.RH, self.RZ = place, Y, PR, RX, RH, RZ
+        self.py_s, self.py_r, self.h_s, self.h_r, self.w_s, self.w_r, self.rz_s, self.rz_r = sems
+        self.half = Y.shape[-1] // 2
+
+    @staticmethod
+    def sems():
+        dma = pltpu.SemaphoreType.DMA
+        return [
+            dma((4, 4)), dma((4, 4)), dma((2, 4)), dma((2, 4)), dma((2, 4, 2)), dma((2, 4, 2)), dma((3,)), dma((3,)),
+        ]
+
+    def copy(self, src, dst, send, recv, to):
+        return pltpu.make_async_remote_copy(
+            src_ref=src, dst_ref=dst, send_sem=send, recv_sem=recv, device_id=to, device_id_type=MESH
+        )
+
+    def pair(self, r, q):
+        src = self.Y.at[self.p.cols[r], self.p.zs[q], 1 - self.p.c]
+        return self.copy(src, self.PR.at[r, q], self.py_s.at[r, q], self.py_r.at[r, q], self.p.partner())
+
+    def cols(self, n):
+        return pl.ds(n * self.half, self.half)
+
+    def through(self, way, q):
+        src = self.Y.at[self.p.cols[3], self.p.zs[q], self.p.c, :, self.cols(1 - way)]
+        return self.copy(src, self.RH.at[way, q], self.h_s.at[way, q], self.h_r.at[way, q], self.p.side(way))
+
+    def beside(self, way, q, n):
+        r = 2 - way
+        src = self.Y.at[self.p.cols[r], self.p.zs[q], self.p.c, :, self.cols(n)]
+        dst = self.RX.at[way, q, :, self.cols(n)]
+        return self.copy(src, dst, self.w_s.at[way, q, n], self.w_r.at[way, q, n], self.p.side(way))
+
+    def to_z(self, k):
+        src = self.Y.at[self.p.cols[0], self.p.zs[k], self.p.c]
+        return self.copy(src, self.RZ.at[k - 1], self.rz_s.at[k - 1], self.rz_r.at[k - 1], self.p.zpeer(k))
+
+    def first(self, q):
+        p = self.p
+        for r in (3, 1, 2, 0):
+            self.pair(r, q).wait_recv()
+            at = (p.cols[r], p.zs[q], p.c)
+            self.Y[at] = (self.Y[at].astype(jnp.float32) + self.PR[r, q].astype(jnp.float32)).astype(jnp.bfloat16)
+            if r == 3:
+                self.through(0, q).start()
+                self.through(1, q).start()
+            if r == 1:
+                self.beside(1, q, 1).start()
+            if r == 2:
+                self.beside(0, q, 0).start()
+
+    def second(self, q):
+        p = self.p
+        for way in (1, 0):
+            n = 1 - way
+            self.through(way, q).wait_recv()
+            at = (p.cols[2 - way], p.zs[q], p.c, slice(None), self.cols(n))
+            self.Y[at] = (self.Y[at].astype(jnp.float32) + self.RH[way, q].astype(jnp.float32)).astype(jnp.bfloat16)
+            self.beside(way, q, n).start()
+
+    def third(self, q):
+        p = self.p
+        for way in (0, 1):
+            for n in (0, 1):
+                self.beside(way, q, n).wait_recv()
+        if q:
+            at = (p.cols[0], p.zs[q], p.c)
+            total = self.Y[at].astype(jnp.float32) + self.RX[0, q].astype(jnp.float32) + self.RX[1, q].astype(jnp.float32)
+            self.Y[at] = total.astype(jnp.bfloat16)
+            self.to_z(q).start()
+
+    def total(self):
+        p = self.p
+        for k in (1, 2, 3):
+            self.to_z(k).wait_recv()
+        at = (p.cols[0], p.zs[0], p.c)
+        total = self.Y[at].astype(jnp.float32) + self.RX[0, 0].astype(jnp.float32) + self.RX[1, 0].astype(jnp.float32)
+        for k in range(3):
+            total = total + self.RZ[k].astype(jnp.float32)
+        return total
+
+    def finish(self):
+        for k in (1, 2, 3):
+            self.to_z(k).wait_send()
+        for q in range(4):
+            for way in (0, 1):
+                self.through(way, q).wait_send()
+                for n in (0, 1):
+                    self.beside(way, q, n).wait_send()
+            for r in range(4):
+                self.pair(r, q).wait_send()
+
+
+def ffn_kernel(x_ref, wg_ref, wu_ref, wd_ref, out_ref, X, Y, WG, WU, WD, H, PR, RX, RH, RZ, local, *sems):
+    p = Place()
+    gather = Gather(p, X, sems[:8])
+    reduce = Reduce(p, Y, PR, RX, RH, RZ, sems[8:])
+    own = pltpu.make_async_copy(x_ref, gather.block(0, 0, p.c), local.at[0])
+    loads = [
+        pltpu.make_async_copy(ref.at[0], buf, local.at[1 + i])
+        for i, (ref, buf) in enumerate(((wg_ref, WG), (wu_ref, WU), (wd_ref, WD)))
+    ]
+    own.start()
+    for load in loads:
+        load.start()
+    enter(p.peers())
+    own.wait()
+    gather.start()
+    gather.spread_z(1)
+    rows = X.shape[-2]
+    model = X.shape[-1]
+    tile = min(512, model)
+    order = ((0, 0), (1, 0), (2, 0), (0, 1), (3, 0), (1, 1), (2, 1), (3, 1))
+
+    def before(i):
+        if i == 0:
+            gather.spread_x(0)
+            for load in loads:
+                load.wait()
+        if i == 1:
+            gather.spread_z(2)
+            gather.spread_x(1)
+        if i == 3:
+            gather.spread_z(3)
+        if i == 4:
+            gather.spread_x2(0)
+            gather.spread_x2(1)
+            gather.spread_x(2)
+        if i == 5:
+            gather.spread_x(3)
+        if i == 6:
+            reduce.first(1)
+        if i == 7:
+            gather.spread_x2(2)
+            gather.spread_x2(3)
+            reduce.second(1)
+        r, b = order[i]
+        gather.need(r, (2 * b, 2 * b + 1))
+
+    def after(i):
+        r, b = order[i]
+        for q in (2 * b, 2 * b + 1):
+            reduce.pair(r, q).start()
+
+    def step(i, carry):
+        for n in range(8):
+            pl.when(i == n)(functools.partial(before, n))
+        r = (i == 1) * 1 + (i == 2) * 2 + (i == 4) * 3 + (i == 5) * 1 + (i == 6) * 2 + (i == 7) * 3
+        b = (i == 3) * 1 + (i >= 5) * 1
+        shift = (r == 1) * 3 + (r == 2) * 1 + (r == 3) * 2
+        col = (p.x + shift) % NX
+        pair = (p.z // 2 + b) % 2
+        zs = pl.ds(2 * pair, 2)
+        value = X[col, zs].reshape(4 * rows, model)
+        gate = jnp.dot(value, WG[...], preferred_element_type=jnp.float32)
+        up = jnp.dot(value, WU[...], preferred_element_type=jnp.float32)
+        H[...] = (gate / (1.0 + jnp.exp(-gate)) * up).astype(jnp.bfloat16)
+
+        def down(n, carry):
+            at = pl.ds(pl.multiple_of(n * tile, tile), tile)
+            part = jnp.dot(H[...], WD[:, at], preferred_element_type=jnp.float32)
+            Y[col, zs, :, :, at] = part.astype(jnp.bfloat16).reshape(2, 2, rows, tile)
+            return carry
+
+        lax.fori_loop(0, model // tile, down, 0)
+        for n in range(8):
+            pl.when(i == n)(functools.partial(after, n))
+        return carry
+
+    lax.fori_loop(0, 8, step, 0)
+    reduce.first(2)
+    reduce.third(1)
+    reduce.first(3)
+    reduce.second(2)
+    reduce.first(0)
+    reduce.second(3)
+    reduce.third(2)
+    reduce.second(0)
+    reduce.third(3)
+    reduce.third(0)
+    out_ref[...] = reduce.total().astype(jnp.bfloat16)
+    gather.finish()
+    reduce.finish()
+
+
+def ffn(inbound, w_gate, w_up, w_down):
+    rows, model = inbound.shape
+    hidden = w_gate.shape[-1]
+    bf16 = jnp.bfloat16
+    any_space = pl.BlockSpec(memory_space=pl.ANY)
+    return pl.pallas_call(
+        ffn_kernel,
+        out_shape=jax.ShapeDtypeStruct((rows, model), bf16),
+        in_specs=[any_space] * 4,
+        out_specs=pl.BlockSpec(memory_space=pltpu.VMEM),
+        scratch_shapes=[
+            pltpu.VMEM((NX, NZ, 2, rows, model), bf16),
+            pltpu.VMEM((NX, NZ, 2, rows, model), bf16),
+            pltpu.VMEM((model, hidden), bf16),
+            pltpu.VMEM((model, hidden), bf16),
+            pltpu.VMEM((hidden, model), bf16),
+            pltpu.VMEM((4 * rows, hidden), bf16),
+            pltpu.VMEM((4, 4, rows, model), bf16),
+            pltpu.VMEM((2, 4, rows, model), bf16),
+            pltpu.VMEM((2, 4, rows, model // 2), bf16),
+            pltpu.VMEM((3, rows, model), bf16),
+            pltpu.SemaphoreType.DMA((4,)),
+            *Gather.sems(),
+            *Reduce.sems(),
+        ],
+        compiler_params=pltpu.CompilerParams(
+            collective_id=0, has_side_effects=True, vmem_limit_bytes=VMEM_LIMIT
+        ),
+        name="ffn",
+    )(inbound, w_gate, w_up, w_down)
+
+
+def kv_kernel(sections, x_ref, w_ref, out_ref, X, S, local, send, recv, *sems):
+    p = Place()
+    gather = Gather(p, X, sems)
+    rows, model = X.shape[-2:]
+    group = NZ * 2 * rows
+    own = pltpu.make_async_copy(x_ref, gather.block(0, 0, p.c), local)
+    own.start()
+    m = lax.axis_index("mp")
+    after = ((p.s + 1) % sections, m)
+    ahead = ((p.s + sections - 1) % sections, m)
+    enter(p.peers() + [after, ahead])
+    own.wait()
+    gather.start()
+
+    def piece(r):
+        at = pl.ds(pl.multiple_of(p.cols[r] * group, group), group)
+        return pltpu.make_async_remote_copy(
+            src_ref=S.at[p.cols[r]], dst_ref=out_ref.at[at], send_sem=send.at[r], recv_sem=recv.at[r],
+            device_id=after, device_id_type=MESH,
+        )
+
+    def product(r):
+        value = X[p.cols[r]].reshape(group, model)
+        S[p.cols[r]] = jnp.dot(value, w_ref[...], preferred_element_type=jnp.float32).astype(jnp.bfloat16)
+        piece(r).start()
+
+    gather.spread_z(1)
+    gather.spread_x(0)
+    gather.spread_z(2)
+    gather.spread_x(1)
+    gather.spread_z(3)
+    gather.spread_x(2)
+    gather.need(0, range(4))
+    product(0)
+    gather.spread_x(3)
+    gather.spread_x2(0)
+    gather.spread_x2(1)
+    gather.need(1, range(4))
+    product(1)
+    gather.need(2, range(4))
+    product(2)
+    gather.spread_x2(2)
+    gather.spread_x2(3)
+    gather.need(3, range(4))
+    product(3)
+    for r in range(4):
+        piece(r).wait_recv()
+    for r in range(4):
+        piece(r).wait_send()
+    gather.finish()
+
+
+def kv_sent(attn_input, w_kv):
+    rows, model = attn_input.shape
+    width = w_kv.shape[1]
+    bf16 = jnp.bfloat16
+    vmem = pl.BlockSpec(memory_space=pltpu.VMEM)
+    return pl.pallas_call(
+        functools.partial(kv_kernel, lax.axis_size("section")),
+        out_shape=jax.ShapeDtypeStruct((NX * NZ * 2 * rows, width), bf16),
+        in_specs=[pl.BlockSpec(memory_space=pl.ANY), vmem],
+        out_specs=vmem,
+        scratch_shapes=[
+            pltpu.VMEM((NX, NZ, 2, rows, model), bf16),
+            pltpu.VMEM((NX, NZ * 2 * rows, width), bf16),
+            pltpu.SemaphoreType.DMA,
+            pltpu.SemaphoreType.DMA((4,)),
+            pltpu.SemaphoreType.DMA((4,)),
+            *Gather.sems(),
+        ],
+        compiler_params=pltpu.CompilerParams(
+            collective_id=1, has_side_effects=True, vmem_limit_bytes=VMEM_LIMIT
+        ),
+        name="kv_sent",
+    )(attn_input, w_kv)
 
 
 def body(stream, ffn_gain, router_weight, expert_ids, w_gate, w_up, w_down, attn_gain, w_kv):
@@ -43,20 +461,7 @@
     ).astype(jnp.bfloat16)
     arrived = lax.all_to_all(buffer, "section", split_axis=0, concat_axis=0, tiled=True)
     inbound = arrived.reshape(experts * capacity, model_width)
-    gate_weight = w_gate[0]
-    up_weight = w_up[0]
-    down_weight = w_down[0]
-    block_rows = lax.all_gather(inbound, "mp", axis=0, tiled=True)
-    gate_part = jnp.dot(block_rows, gate_weight, preferred_element_type=jnp.float32)
-    up_part = jnp.dot(block_rows, up_weight, preferred_element_type=jnp.float32)
-    hidden_all = (jax.nn.silu(gate_part) * up_part).astype(jnp.bfloat16)
-    block_rows = hidden_all
-    summed = lax.psum_scatter(
-        jnp.dot(block_rows, down_weight, preferred_element_type=jnp.float32).astype(jnp.bfloat16),
-        "mp",
-        scatter_dimension=0,
-        tiled=True,
-    )
+    summed = ffn(inbound, w_gate, w_up, w_down)
     results = summed.reshape(experts, capacity, model_width)
     returned = lax.all_to_all(results, "section", split_axis=0, concat_axis=0, tiled=True)
     picked = jnp.einsum("ecr,ecd->rd", route_table, returned, preferred_element_type=jnp.float32)
@@ -68,12 +473,7 @@
     )
     stream_out = updated.astype(jnp.bfloat16)
     attn_input = normalize(stream_out, attn_gain).astype(jnp.bfloat16)
-    kv_local = jnp.dot(
-        lax.all_gather(attn_input, "mp", axis=0, tiled=True),
-        w_kv,
-        preferred_element_type=jnp.float32,
-    ).astype(jnp.bfloat16)
-    kv_decode = shifted(kv_local, "section", 1)
+    kv_decode = kv_sent(attn_input, w_kv)
     return (stream_out, kv_decode)
 
 

time: 429 us -> 236 us (0.55)
  waiting for transfers between devices: 329 us -> 13 us
  Pallas kernels: 0 us -> 181 us
  matrix products: 38.2 us -> 0.72 us
  blocking collectives: 24.8 us -> 0 us
  local copies, waits for them, and re-layouts: 5.75 us -> 21.9 us
  between operations: 13.9 us -> 0.79 us
    pallas_call x0 -> x2, Pallas kernels: none -> 181 us  [the longest x1 132 us: ffn(): pl.pallas_call(ffn_kernel, out_shape=jax.ShapeDtypeStruct((rows, model),...]
    all_gather x2 -> x0, waiting for transfers between devices: 157 us -> none  [the longest x1 80 us: body(): block_rows = lax.all_gather(inbound, 'mp', axis=0, tiled=True)]
    reduce_scatter x1 -> x0, waiting for transfers between devices: 154 us -> none  [body(): lax.psum_scatter(jnp.dot(block_rows, down_weight, preferred_element_type=...]
    dot_general x3 -> x0, matrix products: 37.4 us -> none  [the longest x1 24.2 us: body(): jnp.dot(block_rows, down_weight, preferred_element_type=jnp.float32)]
    all_to_all x1 -> x0, blocking collectives: 24.8 us -> none  [body(): lax.all_to_all(buffer, 'section', split_axis=0, concat_axis=0, tiled=True)]
    unnamed x14 -> x17, local copies, waits for them, and re-layouts: 1.47 us -> 16.7 us
    all_to_all x0 -> x1, starting transfers between devices: none -> 10.8 us  [body(): lax.all_to_all(buffer, 'section', split_axis=0, concat_axis=0, tiled=True)]
    ppermute x1 -> x0, waiting for transfers between devices: 5.61 us -> none  [shifted(): return lax.ppermute(value, axis, pairs)]
  transfers between devices with their start and end apart: 5 -> 2, of which waited for: 5 -> 2; matrix products, arithmetic and copies ran while one was open for 0% -> 6% of each run, Pallas kernels for 0% -> 0%
where the time goes in v1:
time: 236 us; the launch traced here: 235 us
  Pallas kernels  181 us (77%)
  local copies, waits for them, and re-layouts  21.9 us (9%)
  starting transfers between devices  14.3 us (6%)
  waiting for transfers between devices  13 us (6%)
  other arithmetic  3.6 us (2%)
    pallas_call x1, Pallas kernels, ffn(): pl.pallas_call(ffn_kernel, out_shape=jax.ShapeDtypeStruct((rows, model),...  132 us
    pallas_call x1, Pallas kernels, kv_sent(): pl.pallas_call(functools.partial(kv_kernel, lax.axis_size('section')), ou...  49.1 us
    unnamed x17, local copies, waits for them, and re-layouts  16.7 us
    all_to_all x1, waiting for transfers between devices, body(): lax.all_to_all(results, 'section', split_axis=0, concat_axis=0, tiled=True)  11.7 us
    all_to_all x1, starting transfers between devices, body(): lax.all_to_all(buffer, 'section', split_axis=0, concat_axis=0, tiled=True)  10.8 us
  transfers between devices with their start and end apart: 2, of which 2 were waited for; matrix products, arithmetic and copies ran while one was open for 6% of the time, Pallas kernels for 0%

profile of v1, /device:TPU:3, one launch (start us, length us, event | category | flops | bytes accessed | tf_op | source)
XLA Modules:
  0.0 235.4 jit_solution(5660134407203978901)
XLA Ops:
  0.6 0.0 copy-start
  0.6 0.8 copy.42
  1.4 0.1 eq.61
  1.5 0.1 fusion.13
  1.6 0.1 reduce_window_sum.11
  1.7 0.2 select_reduce_fusion
  1.9 1.1 fusion.4
  2.9 1.0 fusion.6
  3.9 0.2 broadcast_in_dim.16
  4.1 0.1 reshape.91
  4.2 0.2 convolution_convert_fusion
  4.5 1.1 copy.43
  5.6 10.8 %all-to-all-start = ((bf16[8,6,4096]{2,1,0:T(8,128)(2,1)}), bf16[8,6,4096]{2,1,0:T(8,128)(2,1)S(1)}, u32[]{:S(2)}, u32[]{:S(2)}) async-start(bf16[8,6,4096]{2,1,0:T(8,128)(2,1)} %copy.43), calls=%async_computation | async-start | bytes 1048576 | tf_op jit(solution)/shard_map/all_to_all | solution.py:462
  16.4 6.4 %copy.44.wg_ref = bf16[1,4096,448]{2,1,0:T(8,128)(2,1)} copy(bf16[1,4096,448]{1,2,0:T(8,128)(2,1)} %param.13) | data formatting | bytes 7340032 | tf_op args[4]
  22.8 6.5 %copy.45.wu_ref = bf16[1,4096,448]{2,1,0:T(8,128)(2,1)} copy(bf16[1,4096,448]{1,2,0:T(8,128)(2,1)} %param.14) | data formatting | bytes 7340032 | tf_op args[5]
  29.3 1.3 all-to-all-done
  30.6 0.9 reshape.88.x_ref
  31.5 132.0 %ffn.1 = bf16[48,4096]{1,0:T(8,128)(2,1)} custom-call(bf16[48,4096]{1,0:T(8,128)(2,1)} %reshape.88.x_ref, bf16[1,4096,448]{2,1,0:T(8,128)(2,1)} %copy.44.wg_ref, bf16[1,4096,448]{2,1,0:T(8,128)(2,1)} %copy.45.wu_ref, bf16[1,448,4096]{2,1,0:T(8,128)(2,1)} %wd_ref.1), custom_call_target="tpu_custom_call" | custom-call | tf_op jit(solution)/shard_map/ffn/pallas_call | solution.py:336
  163.5 0.0 copy-start.5
  163.5 0.0 copy-start.4
  163.5 2.0 reshape.89
  165.5 3.5 %all-to-all-start.1 = ((bf16[8,6,4096]{2,1,0:T(8,128)(2,1)}), bf16[8,6,4096]{2,1,0:T(8,128)(2,1)S(1)}, u32[]{:S(2)}, u32[]{:S(2)}) async-start(bf16[8,6,4096]{2,1,0:T(8,128)(2,1)} %reshape.89), calls=%async_computation.1 | async-start | bytes 1048576 | tf_op jit(solution)/shard_map/all_to_all | solution.py:466
  169.0 1.3 copy.49.w_ref
  170.3 0.1 fusion.20
  170.5 11.7 %all-to-all-done.1 = bf16[8,6,4096]{2,1,0:T(8,128)(2,1)S(1)} async-done(((bf16[8,6,4096]{2,1,0:T(8,128)(2,1)}), bf16[8,6,4096]{2,1,0:T(8,128)(2,1)S(1)}, u32[]{:S(2)}, u32[]{:S(2)}) %all-to-all-start.1) | async-done | bytes 393248 | tf_op jit(solution)/shard_map/all_to_all | solution.py:466
  182.3 0.3 convolution_bitcast_fusion
  182.6 0.3 reshape.90
  182.9 0.6 fusion.19
  183.5 0.4 fusion.1
  183.9 0.7 fusion.3.x_ref
  184.7 49.1 %kv_sent.1 = bf16[512,64]{1,0:T(8,128)(2,1)} custom-call(bf16[16,4096]{1,0:T(8,128)(2,1)} %fusion.3.x_ref, bf16[4096,64]{1,0:T(8,128)(2,1)} %copy.49.w_ref), custom_call_target="tpu_custom_call" | custom-call | tf_op jit(solution)/shard_map/kv_sent/pallas_call | solution.py:420
  233.7 1.6 copy.50
  (15 shorter events, 0.1 us)
Async XLA Ops:
  0.6 169.7 %copy-start = (bf16[4096,8]{0,1:T(8,128)(2,1)S(1)}, bf16[4096,8]{0,1:T(8,128)(2,1)}, u32[]{:S(2)}) copy-start(bf16[4096,8]{0,1:T(8,128)(2,1)} %param.11) | copy-start | bytes 196612
  5.6 25.0 %all-to-all-start = ((bf16[8,6,4096]{2,1,0:T(8,128)(2,1)}), bf16[8,6,4096]{2,1,0:T(8,128)(2,1)S(1)}, u32[]{:S(2)}, u32[]{:S(2)}) async-start(bf16[8,6,4096]{2,1,0:T(8,128)(2,1)} %copy.43), calls=%async_computation | async-start | bytes 1048576 | tf_op jit(solution)/shard_map/all_to_all | solution.py:462
  31.5 137.5 %copy-start.2 = (bf16[4096,64]{0,1:T(8,128)(2,1)S(1)}, bf16[4096,64]{0,1:T(8,128)(2,1)}, u32[]{:S(2)}) copy-start(bf16[4096,64]{0,1:T(8,128)(2,1)} %param.17) | copy-start | bytes 1572868
  163.5 7.0 %copy-start.5 = (s32[16,2]{0,1:T(2,128)S(1)}, s32[16,2]{0,1:T(2,128)}, u32[]{:S(2)}) copy-start(s32[16,2]{0,1:T(2,128)} %param.12) | copy-start | bytes 388
  163.5 20.0 %copy-start.1 = (bf16[16,4096]{1,0:T(8,128)(2,1)S(1)}, bf16[16,4096]{1,0:T(8,128)(2,1)}, u32[]{:S(2)}) copy-start(bf16[16,4096]{1,0:T(8,128)(2,1)} %param.9) | copy-start | bytes 393220
  163.5 20.4 %copy-start.4 = (f32[4096]{0:T(1024)S(1)}, f32[4096]{0:T(1024)}, u32[]{:S(2)}) copy-start(f32[4096]{0:T(1024)} %param.16) | copy-start | bytes 49156
  165.5 16.8 %all-to-all-start.1 = ((bf16[8,6,4096]{2,1,0:T(8,128)(2,1)}), bf16[8,6,4096]{2,1,0:T(8,128)(2,1)S(1)}, u32[]{:S(2)}, u32[]{:S(2)}) async-start(bf16[8,6,4096]{2,1,0:T(8,128)(2,1)} %reshape.89), calls=%async_computation.1 | async-start | bytes 1048576 | tf_op jit(solution)/shard_map/all_to_all | solution.py:466
  183.9 51.5 %copy-start.3 = (bf16[16,4096]{1,0:T(8,128)(2,1)}, bf16[16,4096]{1,0:T(8,128)(2,1)S(1)}, u32[]{:S(2)}) copy-start(bf16[16,4096]{1,0:T(8,128)(2,1)S(1)} %get-tuple-element.11) | copy-start | bytes 393220

commit v2 on v1

--- a/solution.py
+++ b/solution.py
@@ -12,13 +12,6 @@
 NX = 4
 NZ = 4
 VMEM_LIMIT = 66_000_000
-
-
-def normalize(values, scale_gain):
-    floats = values.astype(jnp.float32)
-    return (
-        floats * lax.rsqrt(jnp.mean(floats * floats, axis=-1, keepdims=True) + epsilon) * scale_gain
-    )
 
 
 class Place:
@@ -236,24 +229,143 @@
                 self.pair(r, q).wait_send()
 
 
-def ffn_kernel(x_ref, wg_ref, wu_ref, wd_ref, out_ref, X, Y, WG, WU, WD, H, PR, RX, RH, RZ, local, *sems):
+def dot(a, b):
+    return jnp.dot(a, b, preferred_element_type=jnp.float32)
+
+
+def dot_t(a, b):
+    return lax.dot_general(a, b, (((1,), (1,)), ((), ())), preferred_element_type=jnp.float32)
+
+
+def count(shape, dim):
+    return lax.broadcasted_iota(jnp.int32, shape, dim).astype(jnp.float32)
+
+
+def whole(values, n):
+    return jnp.floor((values + 0.5) * (1.0 / n))
+
+
+def ones(mask):
+    return jnp.where(mask, 1.0, 0.0).astype(jnp.bfloat16)
+
+
+class Slots:
+    def __init__(self, tokens, experts, cap, pieces):
+        self.tokens, self.experts, self.cap, self.pieces = tokens, experts, cap, pieces
+        self.each = pieces * cap
+        self.slots = experts * self.each
+
+    def of_slots(self, v):
+        e = whole(v, self.each)
+        rest = v - e * self.each
+        j = whole(rest, self.cap)
+        return e, j, rest - j * self.cap
+
+    def of_tokens(self, v):
+        j = whole(v, self.tokens)
+        return j, v - j * self.tokens
+
+    def into(self, hit_t):
+        n, q = self.slots, self.pieces * self.tokens
+        before = dot(hit_t, ones(count((self.tokens, self.tokens), 0) < count((self.tokens, self.tokens), 1)))
+        pick = ones(self.of_slots(count((n, self.experts), 0))[0] == count((n, self.experts), 1))
+        wide = ones(count((self.tokens, q), 0) == self.of_tokens(count((self.tokens, q), 1))[1])
+        hits = dot(dot(pick, hit_t).astype(jnp.bfloat16), wide)
+        turn = dot(dot(pick, before.astype(jnp.bfloat16)).astype(jnp.bfloat16), wide)
+        e, j, slot = self.of_slots(count((n, q), 0))
+        jt = self.of_tokens(count((n, q), 1))[0]
+        return ones((hits > 0.5) & (turn == slot) & (j == jt))
+
+    def out_of(self, hit, hit_k):
+        n, q = self.slots, self.pieces * self.tokens
+        before = dot(ones(count((self.tokens, self.tokens), 1) < count((self.tokens, self.tokens), 0)), hit)
+        pick = ones(self.of_slots(count((self.experts, n), 1))[0] == count((self.experts, n), 0))
+        wide = ones(count((q, self.tokens), 1) == self.of_tokens(count((q, self.tokens), 0))[1])
+        e, j, slot = self.of_slots(count((q, n), 1))
+        jt = self.of_tokens(count((q, n), 0))[0]
+        turn = dot(wide, dot(before.astype(jnp.bfloat16), pick).astype(jnp.bfloat16))
+        place = (turn == slot) & (j == jt)
+        return [ones((dot(wide, dot(one, pick).astype(jnp.bfloat16)) > 0.5) & place) for one in hit_k]
+
+    def order(self, back):
+        n = self.slots
+        a, b = (count((n, n), 0), count((n, n), 1)) if not back else (count((n, n), 1), count((n, n), 0))
+        j = whole(a, self.experts * self.cap)
+        rest = a - j * (self.experts * self.cap)
+        s = whole(rest, self.cap)
+        return ones(b == s * self.each + j * self.cap + (rest - s * self.cap))
+
+
+def kernel(
+    sections, cap, pieces,
+    stream_ref, ffn_gain_ref, router_ref, ids_ref, ids_t_ref, wg_ref, wu_ref, wd_ref, attn_gain_ref, wkv_ref,
+    out_ref, kv_ref,
+    X, Y, WG, WU, WD, H, PR, RX, RH, RZ, S, A, R, X2, K, local, d_s, d_r, b_s, b_r, k_s, k_r, *sems,
+):
     p = Place()
+    bf16, f32 = jnp.bfloat16, jnp.float32
     gather = Gather(p, X, sems[:8])
-    reduce = Reduce(p, Y, PR, RX, RH, RZ, sems[8:])
-    own = pltpu.make_async_copy(x_ref, gather.block(0, 0, p.c), local.at[0])
+    reduce = Reduce(p, Y, PR, RX, RH, RZ, sems[8:16])
+    gather2 = Gather(p, X2, sems[16:])
+    tokens, model = stream_ref.shape
+    rows = X.shape[-2]
+    part = model // pieces
+    cut = [slice(j * part, (j + 1) * part) for j in range(pieces)]
+    slots = Slots(tokens, sections, cap, pieces)
     loads = [
-        pltpu.make_async_copy(ref.at[0], buf, local.at[1 + i])
+        pltpu.make_async_copy(ref.at[0], buf, local.at[i])
         for i, (ref, buf) in enumerate(((wg_ref, WG), (wu_ref, WU), (wd_ref, WD)))
     ]
-    own.start()
     for load in loads:
         load.start()
-    enter(p.peers())
-    own.wait()
+
+    def section(d):
+        z = p.z if d % 2 == 0 else NZ - 1 - p.z
+        return ((p.s + d) % sections, p.x * (NZ * 2) + z * 2 + p.c)
+
+    m = lax.axis_index("mp")
+    after = ((p.s + 1) % sections, m)
+    ahead = ((p.s + sections - 1) % sections, m)
+    far = (7, 1, 5, 3, 2, 6, 4)
+    barrier = pltpu.get_barrier_semaphore()
+    peers = p.peers() + [section(d) for d in far] + [after, ahead]
+    for peer in peers:
+        pl.semaphore_signal(barrier, inc=1, device_id=peer, device_id_type=MESH)
+
+    def scaled(values, gain):
+        return values * lax.rsqrt(jnp.mean(values * values, axis=-1, keepdims=True) + epsilon) * gain
+
+    normed = scaled(stream_ref[...].astype(f32), ffn_gain_ref[...]).astype(bf16)
+    e_of = lax.broadcasted_iota(jnp.int32, (sections, tokens), 0)
+    hit_t = ones((e_of == ids_t_ref[0:1, :]) | (e_of == ids_t_ref[1:2, :]))
+    stacked = jnp.concatenate([normed[:, c] for c in cut], axis=0)
+    S[...] = dot(slots.into(hit_t), stacked).astype(bf16).reshape(S.shape)
+
+    def give(src, dst, d, send, recv):
+        return pltpu.make_async_remote_copy(
+            src_ref=src.at[(p.s + d) % sections], dst_ref=dst.at[p.s], send_sem=send.at[d], recv_sem=recv.at[d],
+            device_id=section(d), device_id_type=MESH,
+        )
+
+    pl.semaphore_wait(barrier, len(peers))
+    for d in far:
+        give(S, A, d, d_s, d_r).start()
+    A[p.s] = S[p.s]
+    logits = dot_t(normed, router_ref[...])
+    t_of = lax.broadcasted_iota(jnp.int32, (tokens, sections), 1)
+    named = [t_of == ids_ref[:, k:k + 1] for k in (0, 1)]
+    chosen = [jnp.sum(jnp.where(one, logits, 0.0), axis=-1, keepdims=True) for one in named]
+    share = 1.0 / (1.0 + jnp.exp(chosen[1] - chosen[0]))
+    forth = slots.order(False)
+    for d in far:
+        give(S, A, d, d_s, d_r).wait_recv()
+    block = dot(forth, A[...].reshape(slots.slots, part)).astype(bf16)
+    own = (p.x, p.z, p.c)
+    for j in range(pieces):
+        X[p.x, p.z, p.c, :, cut[j]] = block[j * rows:(j + 1) * rows]
+
     gather.start()
     gather.spread_z(1)
-    rows = X.shape[-2]
-    model = X.shape[-1]
     tile = min(512, model)
     order = ((0, 0), (1, 0), (2, 0), (0, 1), (3, 0), (1, 1), (2, 1), (3, 1))
 
@@ -282,7 +394,7 @@
         r, b = order[i]
         gather.need(r, (2 * b, 2 * b + 1))
 
-    def after(i):
+    def behind(i):
         r, b = order[i]
         for q in (2 * b, 2 * b + 1):
             reduce.pair(r, q).start()
@@ -297,19 +409,18 @@
         pair = (p.z // 2 + b) % 2
         zs = pl.ds(2 * pair, 2)
         value = X[col, zs].reshape(4 * rows, model)
-        gate = jnp.dot(value, WG[...], preferred_element_type=jnp.float32)
-        up = jnp.dot(value, WU[...], preferred_element_type=jnp.float32)
-        H[...] = (gate / (1.0 + jnp.exp(-gate)) * up).astype(jnp.bfloat16)
+        gate = dot_t(value, WG[...])
+        up = dot_t(value, WU[...])
+        H[...] = (gate / (1.0 + jnp.exp(-gate)) * up).astype(bf16)
 
         def down(n, carry):
             at = pl.ds(pl.multiple_of(n * tile, tile), tile)
-            part = jnp.dot(H[...], WD[:, at], preferred_element_type=jnp.float32)
-            Y[col, zs, :, :, at] = part.astype(jnp.bfloat16).reshape(2, 2, rows, tile)
+            Y[col, zs, :, :, at] = dot(H[...], WD[:, at]).astype(bf16).reshape(2, 2, rows, tile)
             return carry
 
         lax.fori_loop(0, model // tile, down, 0)
         for n in range(8):
-            pl.when(i == n)(functools.partial(after, n))
+            pl.when(i == n)(functools.partial(behind, n))
         return carry
 
     lax.fori_loop(0, 8, step, 0)
@@ -323,158 +434,129 @@
     reduce.second(0)
     reduce.third(3)
     reduce.third(0)
-    out_ref[...] = reduce.total().astype(jnp.bfloat16)
+    hit_k = [ones(one) for one in named]
+    fetch = slots.out_of(ones(named[0] | named[1]), hit_k)
+    sums = reduce.total().astype(bf16)
+    for d in far:
+        give(S, A, d, d_s, d_r).wait_send()
+    packed = dot(slots.order(True), jnp.concatenate([sums[:, c] for c in cut], axis=0)).astype(bf16)
+    S[...] = packed.reshape(S.shape)
+    for d in far:
+        give(S, R, d, b_s, b_r).start()
+    R[p.s] = S[p.s]
+    for d in far:
+        give(S, R, d, b_s, b_r).wait_recv()
+    back = R[...].reshape(slots.slots, part)
+    share = jnp.concatenate([share] * pieces, axis=0)
+    base = jnp.concatenate([stream_ref[:, c].astype(f32) for c in cut], axis=0)
+    updated = (base + share * dot(fetch[0], back) + (1.0 - share) * dot(fetch[1], back)).astype(bf16)
+    floats = updated.astype(f32)
+    squares = jnp.sum(floats * floats, axis=-1, keepdims=True)
+    total = squares[0:tokens]
+    for j in range(1, pieces):
+        total = total + squares[j * tokens:(j + 1) * tokens]
+    scale = lax.rsqrt(total * (1.0 / model) + epsilon)
+    for j in range(pieces):
+        at = slice(j * tokens, (j + 1) * tokens)
+        X2[p.x, p.z, p.c, :, cut[j]] = (floats[at] * scale * attn_gain_ref[:, cut[j]]).astype(bf16)
+    gather2.start()
+    for j in range(pieces):
+        out_ref[:, cut[j]] = updated[j * tokens:(j + 1) * tokens]
+
+    group = NZ * 2 * tokens
+
+    def piece(r):
+        at = pl.ds(pl.multiple_of(p.cols[r] * group, group), group)
+        return pltpu.make_async_remote_copy(
+            src_ref=K.at[p.cols[r]], dst_ref=kv_ref.at[:, at], send_sem=k_s.at[r], recv_sem=k_r.at[r],
+            device_id=after, device_id_type=MESH,
+        )
+
+    def product(r):
+        gather2.need(r, range(4))
+        K[p.cols[r]] = dot_t(wkv_ref[...], X2[p.cols[r]].reshape(group, model)).astype(bf16)
+        piece(r).start()
+
+    gather2.spread_z(1)
+    gather2.spread_x(0)
+    gather2.spread_z(2)
+    gather2.spread_x(1)
+    gather2.spread_z(3)
+    gather2.spread_x(2)
+    gather2.spread_x2(0)
+    product(0)
+    gather2.spread_x(3)
+    gather2.spread_x2(1)
+    product(1)
+    gather2.spread_x2(2)
+    product(2)
+    gather2.spread_x2(3)
+    product(3)
     gather.finish()
     reduce.finish()
-
-
-def ffn(inbound, w_gate, w_up, w_down):
-    rows, model = inbound.shape
+    gather2.finish()
+    for d in far:
+        give(S, R, d, b_s, b_r).wait_send()
+    for r in range(4):
+        piece(r).wait_recv()
+    for r in range(4):
+        piece(r).wait_send()
+
+
+def body(stream, ffn_gain, router_weight, expert_ids, w_gate, w_up, w_down, attn_gain, w_kv):
+    tokens, model = stream.shape
+    sections = lax.axis_size("section")
+    cap = min(tokens, 3 * tokens // router_weight.shape[1])
+    pieces = 8
+    rows = sections * cap
     hidden = w_gate.shape[-1]
+    width = w_kv.shape[1]
+    part = model // pieces
     bf16 = jnp.bfloat16
+    dma = pltpu.SemaphoreType.DMA
     any_space = pl.BlockSpec(memory_space=pl.ANY)
-    return pl.pallas_call(
-        ffn_kernel,
-        out_shape=jax.ShapeDtypeStruct((rows, model), bf16),
-        in_specs=[any_space] * 4,
-        out_specs=pl.BlockSpec(memory_space=pltpu.VMEM),
+    vmem = pl.BlockSpec(memory_space=pltpu.VMEM)
+    exchange = pltpu.VMEM((sections, pieces * cap, part), bf16)
+    stream_out, kv_t = pl.pallas_call(
+        functools.partial(kernel, sections, cap, pieces),
+        out_shape=(
+            jax.ShapeDtypeStruct((tokens, model), bf16),
+            jax.ShapeDtypeStruct((width, NX * NZ * 2 * tokens), bf16),
+        ),
+        in_specs=[vmem] * 5 + [any_space] * 3 + [vmem] * 2,
+        out_specs=(vmem, vmem),
         scratch_shapes=[
             pltpu.VMEM((NX, NZ, 2, rows, model), bf16),
             pltpu.VMEM((NX, NZ, 2, rows, model), bf16),
-            pltpu.VMEM((model, hidden), bf16),
-            pltpu.VMEM((model, hidden), bf16),
+            pltpu.VMEM((hidden, model), bf16),
+            pltpu.VMEM((hidden, model), bf16),
             pltpu.VMEM((hidden, model), bf16),
             pltpu.VMEM((4 * rows, hidden), bf16),
             pltpu.VMEM((4, 4, rows, model), bf16),
             pltpu.VMEM((2, 4, rows, model), bf16),
             pltpu.VMEM((2, 4, rows, model // 2), bf16),
             pltpu.VMEM((3, rows, model), bf16),
-            pltpu.SemaphoreType.DMA((4,)),
+            exchange,
+            exchange,
+            exchange,
+            pltpu.VMEM((NX, NZ, 2, tokens, model), bf16),
+            pltpu.VMEM((NX, width, NZ * 2 * tokens), bf16),
+            dma((3,)),
+            dma((8,)), dma((8,)), dma((8,)), dma((8,)),
+            dma((4,)), dma((4,)),
             *Gather.sems(),
             *Reduce.sems(),
+            *Gather.sems(),
         ],
         compiler_params=pltpu.CompilerParams(
             collective_id=0, has_side_effects=True, vmem_limit_bytes=VMEM_LIMIT
         ),
-        name="ffn",
-    )(inbound, w_gate, w_up, w_down)
-
-
-def kv_kernel(sections, x_ref, w_ref, out_ref, X, S, local, send, recv, *sems):
-    p = Place()
-    gather = Gather(p, X, sems)
-    rows, model = X.shape[-2:]
-    group = NZ * 2 * rows
-    own = pltpu.make_async_copy(x_ref, gather.block(0, 0, p.c), local)
-    own.start()
-    m = lax.axis_index("mp")
-    after = ((p.s + 1) % sections, m)
-    ahead = ((p.s + sections - 1) % sections, m)
-    enter(p.peers() + [after, ahead])
-    own.wait()
-    gather.start()
-
-    def piece(r):
-        at = pl.ds(pl.multiple_of(p.cols[r] * group, group), group)
-        return pltpu.make_async_remote_copy(
-            src_ref=S.at[p.cols[r]], dst_ref=out_ref.at[at], send_sem=send.at[r], recv_sem=recv.at[r],
-            device_id=after, device_id_type=MESH,
-        )
-
-    def product(r):
-        value = X[p.cols[r]].reshape(group, model)
-        S[p.cols[r]] = jnp.dot(value, w_ref[...], preferred_element_type=jnp.float32).astype(jnp.bfloat16)
-        piece(r).start()
-
-    gather.spread_z(1)
-    gather.spread_x(0)
-    gather.spread_z(2)
-    gather.spread_x(1)
-    gather.spread_z(3)
-    gather.spread_x(2)
-    gather.need(0, range(4))
-    product(0)
-    gather.spread_x(3)
-    gather.spread_x2(0)
-    gather.spread_x2(1)
-    gather.need(1, range(4))
-    product(1)
-    gather.need(2, range(4))
-    product(2)
-    gather.spread_x2(2)
-    gather.spread_x2(3)
-    gather.need(3, range(4))
-    product(3)
-    for r in range(4):
-        piece(r).wait_recv()
-    for r in range(4):
-        piece(r).wait_send()
-    gather.finish()
-
-
-def kv_sent(attn_input, w_kv):
-    rows, model = attn_input.shape
-    width = w_kv.shape[1]
-    bf16 = jnp.bfloat16
-    vmem = pl.BlockSpec(memory_space=pltpu.VMEM)
-    return pl.pallas_call(
-        functools.partial(kv_kernel, lax.axis_size("section")),
-        out_shape=jax.ShapeDtypeStruct((NX * NZ * 2 * rows, width), bf16),
-        in_specs=[pl.BlockSpec(memory_space=pl.ANY), vmem],
-        out_specs=vmem,
-        scratch_shapes=[
-            pltpu.VMEM((NX, NZ, 2, rows, model), bf16),
-            pltpu.VMEM((NX, NZ * 2 * rows, width), bf16),
-            pltpu.SemaphoreType.DMA,
-            pltpu.SemaphoreType.DMA((4,)),
-            pltpu.SemaphoreType.DMA((4,)),
-            *Gather.sems(),
-        ],
-        compiler_params=pltpu.CompilerParams(
-            collective_id=1, has_side_effects=True, vmem_limit_bytes=VMEM_LIMIT
-        ),
-        name="kv_sent",
-    )(attn_input, w_kv)
-
-
-def body(stream, ffn_gain, router_weight, expert_ids, w_gate, w_up, w_down, attn_gain, w_kv):
-    own_rows = stream.shape[0]
-    model_width = stream.shape[1]
-    experts = router_weight.shape[1]
-    capacity = min(own_rows, 3 * own_rows // experts)
-    normed = normalize(stream, ffn_gain).astype(jnp.bfloat16)
-    logits = jnp.dot(normed, router_weight, preferred_element_type=jnp.float32)
-    onehot = expert_ids[:, :, None] == jnp.arange(experts, dtype=jnp.int32)[None, None, :]
-    chosen = jnp.sum(jnp.where(onehot, logits[:, None, :], jnp.float32(0.0)), axis=-1)
-    share_first = jax.nn.sigmoid(chosen[:, 0] - chosen[:, 1])
-    flat_hits = onehot.reshape(own_rows * 2, experts).astype(jnp.int32)
-    before = jnp.cumsum(flat_hits, axis=0) - flat_hits
-    slot_index = jnp.sum(before * flat_hits, axis=-1)
-    expert_flat = expert_ids.reshape(-1)
-    route_table = (
-        expert_flat[None, None, :] == jnp.arange(experts, dtype=jnp.int32)[:, None, None]
-    ) & (slot_index[None, None, :] == jnp.arange(capacity, dtype=jnp.int32)[None, :, None])
-    route_table = route_table.astype(jnp.bfloat16)
-    repeated = jnp.repeat(normed, 2, axis=0)
-    buffer = jnp.einsum(
-        "ecr,rd->ecd", route_table, repeated, preferred_element_type=jnp.float32
-    ).astype(jnp.bfloat16)
-    arrived = lax.all_to_all(buffer, "section", split_axis=0, concat_axis=0, tiled=True)
-    inbound = arrived.reshape(experts * capacity, model_width)
-    summed = ffn(inbound, w_gate, w_up, w_down)
-    results = summed.reshape(experts, capacity, model_width)
-    returned = lax.all_to_all(results, "section", split_axis=0, concat_axis=0, tiled=True)
-    picked = jnp.einsum("ecr,ecd->rd", route_table, returned, preferred_element_type=jnp.float32)
-    picked = picked.reshape(own_rows, 2, model_width)
-    updated = (
-        stream.astype(jnp.float32)
-        + share_first[:, None] * picked[:, 0]
-        + (1.0 - share_first)[:, None] * picked[:, 1]
+        name="layer",
+    )(
+        stream, ffn_gain[None, :], router_weight.T, expert_ids, expert_ids.T,
+        jnp.swapaxes(w_gate, 1, 2), jnp.swapaxes(w_up, 1, 2), w_down, attn_gain[None, :], w_kv.T,
     )
-    stream_out = updated.astype(jnp.bfloat16)
-    attn_input = normalize(stream_out, attn_gain).astype(jnp.bfloat16)
-    kv_decode = kv_sent(attn_input, w_kv)
-    return (stream_out, kv_decode)
+    return (stream_out, kv_t.T)
 
 
 def solution(mesh):

time: 236 us -> 200 us (0.85)
  local copies, waits for them, and re-layouts: 21.9 us -> 4.4 us
  starting transfers between devices: 14.3 us -> 0 us
  waiting for transfers between devices: 13 us -> 0 us
  Pallas kernels: 181 us -> 192 us
  other arithmetic: 3.6 us -> 0 us
    all_to_all x2 -> x0, starting transfers between devices: 14.3 us -> none  [the longest x1 10.8 us: body(): lax.all_to_all(buffer, 'section', split_axis=0, concat_axis=0, tiled=True)]
    all_to_all x2 -> x0, waiting for transfers between devices: 13 us -> none  [the longest x1 11.7 us: body(): lax.all_to_all(results, 'section', split_axis=0, concat_axis=0, tiled=True)]
    unnamed x17 -> x3, local copies, waits for them, and re-layouts: 16.7 us -> 4.4 us
    pallas_call x2 -> x1, Pallas kernels: 181 us -> 192 us  [body(): pl.pallas_call(functools.partial(kernel, sections, cap, pieces), out_shap...]
    reshape x4 -> x0, local copies, waits for them, and re-layouts: 3.31 us -> none  [the longest x1 1.98 us: body(): results = summed.reshape(experts, capacity, model_width)]
  transfers between devices with their start and end apart: 2 -> 0, of which waited for: 2 -> 0; matrix products, arithmetic and copies ran while one was open for 6% -> 0% of each run, Pallas kernels for 0% -> 0%
where the time goes in v2:
time: 200 us; the launch traced here: 197 us
  Pallas kernels  192 us (96%)
  local copies, waits for them, and re-layouts  4.4 us (2%)
    pallas_call x1, Pallas kernels, body(): pl.pallas_call(functools.partial(kernel, sections, cap, pieces), out_shap...  192 us
    unnamed x3, local copies, waits for them, and re-layouts  4.4 us

profile of v2, /device:TPU:3, one launch (start us, length us, event | category | flops | bytes accessed | tf_op | source)
XLA Modules:
  0.0 197.1 jit_solution(3033962862458208052)
XLA Ops:
  0.6 1.4 copy.11.ids_ref
  2.0 192.0 %layer.1 = (bf16[16,4096]{1,0:T(8,128)(2,1)}, bf16[64,512]{1,0:T(8,128)(2,1)}) custom-call(bf16[16,4096]{1,0:T(8,128)(2,1)} %stream_ref.1, f32[1,4096]{1,0:T(1,128)} %bitcast.13, bf16[8,4096]{1,0:T(8,128)(2,1)} %bitcast.11, s32[16,2]{1,0:T(8,128)} %copy.11.ids_ref, s32[2,16]{1,0:T(2,128)} %bitcast.15, bf16[1,448,4096]{2,1,0:T(8,128)(2,1)} %bitcast.8, ...), custom_call_target="tpu_custom_call" | custom-call | tf_op jit(solution)/shard_map/layer/pallas_call | solution.py:520
  194.0 1.6 copy.14
  195.6 1.5 copy.15

commit v3 on v2

--- a/solution.py
+++ b/solution.py
@@ -41,16 +41,28 @@
         return [self.partner(), self.side(0), self.side(1)] + [self.zpeer(k) for k in (1, 2, 3)]
 
 
+def mid_of(model):
+    return model * 5 // 32
+
+
+def half_of(way, half, mid):
+    return pl.ds(way * (half + mid), half - mid)
+
+
 class Gather:
     def __init__(self, place, X, sems):
         self.p, self.X = place, X
-        self.zs_s, self.zs_r, self.xs_s, self.xs_r, self.x2_s, self.x2_r, self.p_s, self.p_r = sems
+        self.zs_s, self.zs_r, self.xs_s, self.xs_r, self.x2_s, self.x2_r, self.p_s, self.p_r, self.m_s, self.m_r = sems
         self.half = X.shape[-1] // 2
+        self.mid = mid_of(X.shape[-1])
 
     @staticmethod
     def sems():
         dma = pltpu.SemaphoreType.DMA
-        return [dma((3,)), dma((3,)), dma((2, 4)), dma((2, 4)), dma((2, 4)), dma((2, 4)), dma((4, 4)), dma((4, 4))]
+        return [
+            dma((3,)), dma((3,)), dma((2, 4)), dma((2, 4)), dma((2, 4)), dma((2, 4)), dma((4, 4)), dma((4, 4)),
+            dma((3,)), dma((3,)),
+        ]
 
     def block(self, r, q, c):
         return self.X.at[self.p.cols[r], self.p.zs[q], c]
@@ -73,7 +85,15 @@
         return self.copy(self.block(1 + way, q, self.p.c), self.xs_s.at[way, q], self.xs_r.at[way, q], self.p.side(way))
 
     def part(self, r, q, way):
-        return self.X.at[self.p.cols[r], self.p.zs[q], self.p.c, :, pl.ds(way * self.half, self.half)]
+        return self.X.at[self.p.cols[r], self.p.zs[q], self.p.c, :, half_of(way, self.half, self.mid if q else 0)]
+
+    def to_zmid(self, k):
+        ref = self.X.at[self.p.cols[3], self.p.zs[0], self.p.c, :, pl.ds(self.half - self.mid, 2 * self.mid)]
+        return self.copy(ref, self.m_s.at[k - 1], self.m_r.at[k - 1], self.p.zpeer(k))
+
+    def from_zmid(self, k):
+        ref = self.X.at[self.p.cols[3], self.p.zs[k], self.p.c, :, pl.ds(self.half - self.mid, 2 * self.mid)]
+        return self.copy(ref, self.m_s.at[k - 1], self.m_r.at[k - 1], self.p.zpeer(k))
 
     def on_x(self, way, q):
         return self.copy(self.part(1 + way, q, way), self.x2_s.at[way, q], self.x2_r.at[way, q], self.p.side(way))
@@ -110,6 +130,11 @@
     def spread_x2(self, q):
         for way in (0, 1):
             self.from_x2(way, q).wait_recv()
+        if q:
+            self.from_zmid(q).wait_recv()
+        else:
+            for k in (1, 2, 3):
+                self.to_zmid(k).start()
         self.pair(3, q).start()
 
     def need(self, r, qs):
@@ -119,6 +144,7 @@
     def finish(self):
         for k in (1, 2, 3):
             self.to_z(k).wait_send()
+            self.to_zmid(k).wait_send()
         for q in range(4):
             for way in (0, 1):
                 self.to_x(way, q).wait_send()
@@ -135,16 +161,18 @@
 
 
 class Reduce:
-    def __init__(self, place, Y, PR, RX, RH, RZ, sems):
-        self.p, self.Y, self.PR, self.RX, self.RH, self.RZ = place, Y, PR, RX, RH, RZ
-        self.py_s, self.py_r, self.h_s, self.h_r, self.w_s, self.w_r, self.rz_s, self.rz_r = sems
+    def __init__(self, place, Y, PR, RX, RH, RZ, RM, sems):
+        self.p, self.Y, self.PR, self.RX, self.RH, self.RZ, self.RM = place, Y, PR, RX, RH, RZ, RM
+        self.py_s, self.py_r, self.h_s, self.h_r, self.w_s, self.w_r, self.rz_s, self.rz_r, self.m_s, self.m_r = sems
         self.half = Y.shape[-1] // 2
+        self.mid = mid_of(Y.shape[-1])
 
     @staticmethod
     def sems():
         dma = pltpu.SemaphoreType.DMA
         return [
             dma((4, 4)), dma((4, 4)), dma((2, 4)), dma((2, 4)), dma((2, 4, 2)), dma((2, 4, 2)), dma((3,)), dma((3,)),
+            dma((3,)), dma((3,)),
         ]
 
     def copy(self, src, dst, send, recv, to):
@@ -160,8 +188,17 @@
         return pl.ds(n * self.half, self.half)
 
     def through(self, way, q):
-        src = self.Y.at[self.p.cols[3], self.p.zs[q], self.p.c, :, self.cols(1 - way)]
-        return self.copy(src, self.RH.at[way, q], self.h_s.at[way, q], self.h_r.at[way, q], self.p.side(way))
+        at = half_of(1 - way, self.half, self.mid if q else 0)
+        src = self.Y.at[self.p.cols[3], self.p.zs[q], self.p.c, :, at]
+        dst = self.RH.at[q, :, at]
+        return self.copy(src, dst, self.h_s.at[way, q], self.h_r.at[way, q], self.p.side(way))
+
+    def middle(self):
+        return pl.ds(self.half - self.mid, 2 * self.mid)
+
+    def to_zmid(self, k):
+        src = self.Y.at[self.p.cols[3], self.p.zs[k], self.p.c, :, self.middle()]
+        return self.copy(src, self.RM.at[k - 1], self.m_s.at[k - 1], self.m_r.at[k - 1], self.p.zpeer(k))
 
     def beside(self, way, q, n):
         r = 2 - way
@@ -180,6 +217,16 @@
             at = (p.cols[r], p.zs[q], p.c)
             self.Y[at] = (self.Y[at].astype(jnp.float32) + self.PR[r, q].astype(jnp.float32)).astype(jnp.bfloat16)
             if r == 3:
+                if q:
+                    self.to_zmid(q).start()
+                else:
+                    for k in (1, 2, 3):
+                        self.to_zmid(k).wait_recv()
+                    mid = (p.cols[r], p.zs[q], p.c, slice(None), self.middle())
+                    total = self.Y[mid].astype(jnp.float32)
+                    for k in range(3):
+                        total = total + self.RM[k].astype(jnp.float32)
+                    self.Y[mid] = total.astype(jnp.bfloat16)
                 self.through(0, q).start()
                 self.through(1, q).start()
             if r == 1:
@@ -192,8 +239,9 @@
         for way in (1, 0):
             n = 1 - way
             self.through(way, q).wait_recv()
-            at = (p.cols[2 - way], p.zs[q], p.c, slice(None), self.cols(n))
-            self.Y[at] = (self.Y[at].astype(jnp.float32) + self.RH[way, q].astype(jnp.float32)).astype(jnp.bfloat16)
+            part = half_of(n, self.half, self.mid if q else 0)
+            at = (p.cols[2 - way], p.zs[q], p.c, slice(None), part)
+            self.Y[at] = (self.Y[at].astype(jnp.float32) + self.RH[q, :, part].astype(jnp.float32)).astype(jnp.bfloat16)
             self.beside(way, q, n).start()
 
     def third(self, q):
@@ -220,6 +268,7 @@
     def finish(self):
         for k in (1, 2, 3):
             self.to_z(k).wait_send()
+            self.to_zmid(k).wait_send()
         for q in range(4):
             for way in (0, 1):
                 self.through(way, q).wait_send()
@@ -298,15 +347,15 @@
 
 def kernel(
     sections, cap, pieces,
-    stream_ref, ffn_gain_ref, router_ref, ids_ref, ids_t_ref, wg_ref, wu_ref, wd_ref, attn_gain_ref, wkv_ref,
+    stream_ref, ffn_gain_ref, router_ref, ids_t_ref, wg_ref, wu_ref, wd_ref, attn_gain_ref, wkv_ref,
     out_ref, kv_ref,
-    X, Y, WG, WU, WD, H, PR, RX, RH, RZ, S, A, R, X2, K, local, d_s, d_r, b_s, b_r, k_s, k_r, *sems,
+    X, Y, WG, WU, WD, H, PR, RX, RH, RZ, RM, S, A, R, X2, WK, K, KR,
+    local, d_s, d_r, b_s, b_r, k_s, k_r, wz_s, wz_r, wy_s, wy_r, n_s, n_r, n2_s, n2_r, np_s, np_r, *sems,
 ):
     p = Place()
     bf16, f32 = jnp.bfloat16, jnp.float32
-    gather = Gather(p, X, sems[:8])
-    reduce = Reduce(p, Y, PR, RX, RH, RZ, sems[8:16])
-    gather2 = Gather(p, X2, sems[16:])
+    gather = Gather(p, X, sems[:10])
+    reduce = Reduce(p, Y, PR, RX, RH, RZ, RM, sems[10:])
     tokens, model = stream_ref.shape
     rows = X.shape[-2]
     part = model // pieces
@@ -318,17 +367,20 @@
     ]
     for load in loads:
         load.start()
+    own_wkv = pltpu.make_async_copy(wkv_ref, WK.at[p.z], local.at[3])
+    own_wkv.start()
 
     def section(d):
         z = p.z if d % 2 == 0 else NZ - 1 - p.z
         return ((p.s + d) % sections, p.x * (NZ * 2) + z * 2 + p.c)
 
-    m = lax.axis_index("mp")
-    after = ((p.s + 1) % sections, m)
-    ahead = ((p.s + sections - 1) % sections, m)
+    def next_at(k, d):
+        return ((p.s + d) % sections, p.x * (NZ * 2) + p.zs[k] * 2 + p.c)
+
     far = (7, 1, 5, 3, 2, 6, 4)
     barrier = pltpu.get_barrier_semaphore()
-    peers = p.peers() + [section(d) for d in far] + [after, ahead]
+    peers = p.peers() + [section(d) for d in far]
+    peers = peers + [next_at(k, d) for k in (0, 1, 2) for d in (1, sections - 1)]
     for peer in peers:
         pl.semaphore_signal(barrier, inc=1, device_id=peer, device_id_type=MESH)
 
@@ -352,8 +404,8 @@
         give(S, A, d, d_s, d_r).start()
     A[p.s] = S[p.s]
     logits = dot_t(normed, router_ref[...])
-    t_of = lax.broadcasted_iota(jnp.int32, (tokens, sections), 1)
-    named = [t_of == ids_ref[:, k:k + 1] for k in (0, 1)]
+    same = ones(count((tokens, tokens), 0) == count((tokens, tokens), 1))
+    named = [dot_t(same, ones(e_of == ids_t_ref[k:k + 1, :])) > 0.5 for k in (0, 1)]
     chosen = [jnp.sum(jnp.where(one, logits, 0.0), axis=-1, keepdims=True) for one in named]
     share = 1.0 / (1.0 + jnp.exp(chosen[1] - chosen[0]))
     forth = slots.order(False)
@@ -367,6 +419,22 @@
     gather.start()
     gather.spread_z(1)
     tile = min(512, model)
+
+    y = p.s // 2
+    quarter = model // 4
+
+    def wkv_copy(z, y, send, recv, to):
+        ref = WK.at[z, :, pl.ds(pl.multiple_of(y * quarter, quarter), quarter)]
+        return pltpu.make_async_remote_copy(
+            src_ref=ref, dst_ref=ref, send_sem=send, recv_sem=recv, device_id=to, device_id_type=MESH
+        )
+
+    def wkv_z(k, of):
+        return wkv_copy(p.zs[of], y, wz_s.at[k - 1], wz_r.at[k - 1], p.zpeer(k))
+
+    def wkv_y(k, d, of):
+        return wkv_copy(p.zs[k], (y + of) % 4, wy_s.at[k - 1, d - 1], wy_r.at[k - 1, d - 1], section(2 * d))
+
     order = ((0, 0), (1, 0), (2, 0), (0, 1), (3, 0), (1, 1), (2, 1), (3, 1))
 
     def before(i):
@@ -375,8 +443,8 @@
             for load in loads:
                 load.wait()
         if i == 1:
+            gather.spread_x(1)
             gather.spread_z(2)
-            gather.spread_x(1)
         if i == 3:
             gather.spread_z(3)
         if i == 4:
@@ -385,6 +453,9 @@
             gather.spread_x(2)
         if i == 5:
             gather.spread_x(3)
+            own_wkv.wait()
+            for k in (1, 2, 3):
+                wkv_z(k, 0).start()
         if i == 6:
             reduce.first(1)
         if i == 7:
@@ -429,6 +500,10 @@
     reduce.first(3)
     reduce.second(2)
     reduce.first(0)
+    for k in (1, 2, 3):
+        wkv_z(k, k).wait_recv()
+        for d in (1, 2, 3):
+            wkv_y(k, d, 0).start()
     reduce.second(3)
     reduce.third(2)
     reduce.second(0)
@@ -458,48 +533,78 @@
     scale = lax.rsqrt(total * (1.0 / model) + epsilon)
     for j in range(pieces):
         at = slice(j * tokens, (j + 1) * tokens)
-        X2[p.x, p.z, p.c, :, cut[j]] = (floats[at] * scale * attn_gain_ref[:, cut[j]]).astype(bf16)
-    gather2.start()
+        X2[p.x, p.c, :, cut[j]] = (floats[at] * scale * attn_gain_ref[:, cut[j]]).astype(bf16)
+
+    half = model // 2
+
+    def row(c, r, at, send, recv, to):
+        ref = X2.at[p.cols[r], c, :, at]
+        return pltpu.make_async_remote_copy(
+            src_ref=ref, dst_ref=ref, send_sem=send, recv_sem=recv, device_id=to, device_id_type=MESH
+        )
+
+    every = pl.ds(0, model)
+
+    def row_x(way, r):
+        return row(p.c, r, every, n_s.at[way], n_r.at[way], p.side(way))
+
+    def row_x2(way, r):
+        return row(p.c, r, pl.ds(way * half, half), n2_s.at[way], n2_r.at[way], p.side(way))
+
+    def row_pair(r, c):
+        return row(c, r, every, np_s.at[r], np_r.at[r], p.partner())
+
+    for way in (0, 1):
+        row_x(way, 0).start()
+    row_pair(0, p.c).start()
     for j in range(pieces):
         out_ref[:, cut[j]] = updated[j * tokens:(j + 1) * tokens]
-
-    group = NZ * 2 * tokens
-
-    def piece(r):
-        at = pl.ds(pl.multiple_of(p.cols[r] * group, group), group)
+    for way in (0, 1):
+        row_x(way, 1 + way).wait_recv()
+        row_x2(way, 1 + way).start()
+    for way in (0, 1):
+        row_pair(1 + way, p.c).start()
+    for k in (1, 2, 3):
+        for d in (1, 2, 3):
+            wkv_y(k, d, 4 - d).wait_recv()
+    for way in (0, 1):
+        row_x2(way, 3).wait_recv()
+    row_pair(3, p.c).start()
+    for r in range(4):
+        row_pair(r, 1 - p.c).wait_recv()
+    width = WK.shape[1]
+    each = NX * 2 * tokens
+    K[...] = dot_t(WK[...].reshape(NZ * width, model), X2[...].reshape(each, model)).astype(bf16).reshape(K.shape)
+
+    def piece(k):
         return pltpu.make_async_remote_copy(
-            src_ref=K.at[p.cols[r]], dst_ref=kv_ref.at[:, at], send_sem=k_s.at[r], recv_sem=k_r.at[r],
-            device_id=after, device_id_type=MESH,
+            src_ref=K.at[p.zs[k]], dst_ref=KR.at[p.z], send_sem=k_s.at[k], recv_sem=k_r.at[k],
+            device_id=next_at(k, 1), device_id_type=MESH,
         )
 
-    def product(r):
-        gather2.need(r, range(4))
-        K[p.cols[r]] = dot_t(wkv_ref[...], X2[p.cols[r]].reshape(group, model)).astype(bf16)
-        piece(r).start()
-
-    gather2.spread_z(1)
-    gather2.spread_x(0)
-    gather2.spread_z(2)
-    gather2.spread_x(1)
-    gather2.spread_z(3)
-    gather2.spread_x(2)
-    gather2.spread_x2(0)
-    product(0)
-    gather2.spread_x(3)
-    gather2.spread_x2(1)
-    product(1)
-    gather2.spread_x2(2)
-    product(2)
-    gather2.spread_x2(3)
-    product(3)
+    for k in (3, 1, 2, 0):
+        piece(k).start()
+    a, b = count((NZ * each, NZ * each), 0), count((NZ * each, NZ * each), 1)
+    z_of = whole(a, each)
+    x_of = whole(a - z_of * each, 2 * tokens)
+    t_of = a - z_of * each - x_of * (2 * tokens)
+    into = ones(b == x_of * each + z_of * (2 * tokens) + t_of)
+    for k in range(4):
+        piece(k).wait_recv()
+    kv_ref[...] = dot(jnp.concatenate([KR[z] for z in range(NZ)], axis=1), into).astype(bf16)
     gather.finish()
     reduce.finish()
-    gather2.finish()
+    for k in (1, 2, 3):
+        wkv_z(k, 0).wait_send()
+        for d in (1, 2, 3):
+            wkv_y(k, d, 0).wait_send()
     for d in far:
         give(S, R, d, b_s, b_r).wait_send()
+    for way in (0, 1):
+        row_x(way, 0).wait_send()
+        row_x2(way, 1 + way).wait_send()
     for r in range(4):
-        piece(r).wait_recv()
-    for r in range(4):
+        row_pair(r, p.c).wait_send()
         piece(r).wait_send()
 
 
@@ -523,7 +628,7 @@
             jax.ShapeDtypeStruct((tokens, model), bf16),
             jax.ShapeDtypeStruct((width, NX * NZ * 2 * tokens), bf16),
         ),
-        in_specs=[vmem] * 5 + [any_space] * 3 + [vmem] * 2,
+        in_specs=[vmem] * 4 + [any_space] * 3 + [vmem, any_space],
         out_specs=(vmem, vmem),
         scratch_shapes=[
             pltpu.VMEM((NX, NZ, 2, rows, model), bf16),
@@ -534,26 +639,30 @@
             pltpu.VMEM((4 * rows, hidden), bf16),
             pltpu.VMEM((4, 4, rows, model), bf16),
             pltpu.VMEM((2, 4, rows, model), bf16),
-            pltpu.VMEM((2, 4, rows, model // 2), bf16),
+            pltpu.VMEM((4, rows, model), bf16),
             pltpu.VMEM((3, rows, model), bf16),
+            pltpu.VMEM((3, rows, 2 * mid_of(model)), bf16),
             exchange,
             exchange,
             exchange,
-            pltpu.VMEM((NX, NZ, 2, tokens, model), bf16),
-            pltpu.VMEM((NX, width, NZ * 2 * tokens), bf16),
-            dma((3,)),
+            pltpu.VMEM((NX, 2, tokens, model), bf16),
+            pltpu.VMEM((NZ, width, model), bf16),
+            pltpu.VMEM((NZ, width, NX * 2 * tokens), bf16),
+            pltpu.VMEM((NZ, width, NX * 2 * tokens), bf16),
+            dma((4,)),
             dma((8,)), dma((8,)), dma((8,)), dma((8,)),
             dma((4,)), dma((4,)),
+            dma((3,)), dma((3,)), dma((3, 3)), dma((3, 3)),
+            dma((2,)), dma((2,)), dma((2,)), dma((2,)), dma((4,)), dma((4,)),
             *Gather.sems(),
             *Reduce.sems(),
-            *Gather.sems(),
         ],
         compiler_params=pltpu.CompilerParams(
             collective_id=0, has_side_effects=True, vmem_limit_bytes=VMEM_LIMIT
         ),
         name="layer",
     )(
-        stream, ffn_gain[None, :], router_weight.T, expert_ids, expert_ids.T,
+        stream, ffn_gain[None, :], router_weight.T, expert_ids.T,
         jnp.swapaxes(w_gate, 1, 2), jnp.swapaxes(w_up, 1, 2), w_down, attn_gain[None, :], w_kv.T,
     )
     return (stream_out, kv_t.T)

time: 200 us -> 183 us (0.915); the launches traced: 197 us -> 183 us
  Pallas kernels: 192 us -> 179 us
    pallas_call x1, Pallas kernels: 192 us -> 179 us  [body(): pl.pallas_call(functools.partial(kernel, sections, cap, pieces), out_shap...]
    unnamed x3 -> x2, local copies, waits for them, and re-layouts: 4.4 us -> 3.04 us
where the time goes in v3:
time: 183 us
  Pallas kernels  179 us (98%)
  local copies, waits for them, and re-layouts  3.04 us (2%)
    pallas_call x1, Pallas kernels, body(): pl.pallas_call(functools.partial(kernel, sections, cap, pieces), out_shap...  179 us

profile of v3, /device:TPU:3, one launch (start us, length us, event | category | flops | bytes accessed | tf_op | source)
XLA Modules:
  0.0 182.9 jit_solution(4679385132551776323)
XLA Ops:
  0.6 179.2 %layer.1 = (bf16[16,4096]{1,0:T(8,128)(2,1)}, bf16[64,512]{1,0:T(8,128)(2,1)}) custom-call(bf16[16,4096]{1,0:T(8,128)(2,1)} %stream_ref.1, f32[1,4096]{1,0:T(1,128)} %bitcast.13, bf16[8,4096]{1,0:T(8,128)(2,1)} %bitcast.11, s32[2,16]{1,0:T(2,128)} %bitcast.15, bf16[1,448,4096]{2,1,0:T(8,128)(2,1)} %bitcast.8, bf16[1,448,4096]{2,1,0:T(8,128)(2,1)} %bitcast.9, ...), custom_call_target="tpu_custom_call" | custom-call | tf_op jit(solution)/shard_map/layer/pallas_call | solution.py:625
  179.8 1.6 copy.13
  181.4 1.5 copy.14

commit v4 on v3

--- a/solution.py
+++ b/solution.py
@@ -24,6 +24,8 @@
         z = self.z
         self.cols = [self.x, (self.x + 3) % NX, (self.x + 1) % NX, (self.x + 2) % NX]
         self.zs = [z, z + 1 - 2 * (z % 2), (z + 2) % NZ, NZ - 1 - z]
+        self.inner = (z == 1) | (z == 2)
+        self.zq = [z, z + 1 - 2 * (z % 2), 2 - z // 2, 3 - 3 * (z // 2)]
 
     def at(self, x, z, c):
         return (self.s, x * (NZ * 2) + z * 2 + c)
@@ -43,6 +45,10 @@
 
 def mid_of(model):
     return model * 5 // 32
+
+
+def far_of(model):
+    return model // 4
 
 
 def half_of(way, half, mid):
@@ -52,31 +58,35 @@
 class Gather:
     def __init__(self, place, X, sems):
         self.p, self.X = place, X
-        self.zs_s, self.zs_r, self.xs_s, self.xs_r, self.x2_s, self.x2_r, self.p_s, self.p_r, self.m_s, self.m_r = sems
+        self.zo_s, self.zf_s, self.zs_r, self.xs_s, self.xs_r, self.x2_s, self.x2_r, self.p_s, self.p_r, self.m_s, self.m_r = sems
         self.half = X.shape[-1] // 2
-        self.mid = mid_of(X.shape[-1])
+        self.mid = far_of(X.shape[-1])
 
     @staticmethod
     def sems():
         dma = pltpu.SemaphoreType.DMA
         return [
-            dma((3,)), dma((3,)), dma((2, 4)), dma((2, 4)), dma((2, 4)), dma((2, 4)), dma((4, 4)), dma((4, 4)),
+            dma((2,)), dma((3,)), dma((3,)), dma((2, 4)), dma((2, 4)), dma((2, 4)), dma((2, 4)), dma((4, 4)), dma((4, 4)),
             dma((3,)), dma((3,)),
         ]
 
     def block(self, r, q, c):
-        return self.X.at[self.p.cols[r], self.p.zs[q], c]
+        return self.X.at[self.p.cols[r], self.p.zq[q], c]
 
     def copy(self, ref, send, recv, to):
         return pltpu.make_async_remote_copy(
             src_ref=ref, dst_ref=ref, send_sem=send, recv_sem=recv, device_id=to, device_id_type=MESH
         )
 
-    def to_z(self, k):
-        return self.copy(self.block(0, 0, self.p.c), self.zs_s.at[k - 1], self.zs_r.at[k - 1], self.p.zpeer(k))
-
-    def from_z(self, k):
-        return self.copy(self.block(0, k, self.p.c), self.zs_s.at[k - 1], self.zs_r.at[k - 1], self.p.zpeer(k))
+    def own_z(self, n):
+        return self.copy(self.block(0, 0, self.p.c), self.zo_s.at[n], self.zs_r.at[n], self.p.at(self.p.x, self.p.zq[1 + n], self.p.c))
+
+    def on_z(self, q):
+        to, kind = (2, 3) if q == 1 else (1, q)
+        return self.copy(self.block(0, q, self.p.c), self.zf_s.at[q - 1], self.zs_r.at[kind - 1], self.p.at(self.p.x, self.p.zq[to], self.p.c))
+
+    def from_z(self, q):
+        return self.copy(self.block(0, q, self.p.c), self.zf_s.at[q - 1], self.zs_r.at[q - 1], self.p.partner())
 
     def to_x(self, way, q):
         return self.copy(self.block(0, q, self.p.c), self.xs_s.at[way, q], self.xs_r.at[way, q], self.p.side(way))
@@ -85,7 +95,7 @@
         return self.copy(self.block(1 + way, q, self.p.c), self.xs_s.at[way, q], self.xs_r.at[way, q], self.p.side(way))
 
     def part(self, r, q, way):
-        return self.X.at[self.p.cols[r], self.p.zs[q], self.p.c, :, half_of(way, self.half, self.mid if q else 0)]
+        return self.X.at[self.p.cols[r], self.p.zq[q], self.p.c, :, half_of(way, self.half, self.mid if q else 0)]
 
     def to_zmid(self, k):
         ref = self.X.at[self.p.cols[3], self.p.zs[0], self.p.c, :, pl.ds(self.half - self.mid, 2 * self.mid)]
@@ -110,12 +120,13 @@
     def start(self):
         self.to_x(0, 0).start()
         self.to_x(1, 0).start()
-        for k in (1, 2, 3):
-            self.to_z(k).start()
+        self.own_z(0).start()
+        pl.when(self.p.inner)(lambda: self.own_z(1).start())
         self.pair(0, 0).start()
 
     def spread_z(self, k):
         self.from_z(k).wait_recv()
+        pl.when(self.p.inner)(lambda: self.on_z(k).start())
         self.to_x(0, k).start()
         self.to_x(1, k).start()
         self.pair(0, k).start()
@@ -130,20 +141,33 @@
     def spread_x2(self, q):
         for way in (0, 1):
             self.from_x2(way, q).wait_recv()
-        if q:
-            self.from_zmid(q).wait_recv()
-        else:
+        if q == 0:
             for k in (1, 2, 3):
                 self.to_zmid(k).start()
-        self.pair(3, q).start()
+        if q == 1:
+            self.from_zmid(1).wait_recv()
+        if q < 2:
+            self.pair(3, q).start()
+        if q == 3:
+            for k in (2, 3):
+                self.from_zmid(k).wait_recv()
+            for k in (2, 3):
+                self.pair(3, k).start()
 
     def need(self, r, qs):
         for q in qs:
             self.from_pair(r, q).wait_recv()
 
     def finish(self):
+        self.own_z(0).wait_send()
+
+        def inner():
+            self.own_z(1).wait_send()
+            for q in (1, 2, 3):
+                self.on_z(q).wait_send()
+
+        pl.when(self.p.inner)(inner)
         for k in (1, 2, 3):
-            self.to_z(k).wait_send()
             self.to_zmid(k).wait_send()
         for q in range(4):
             for way in (0, 1):
@@ -210,9 +234,9 @@
         src = self.Y.at[self.p.cols[0], self.p.zs[k], self.p.c]
         return self.copy(src, self.RZ.at[k - 1], self.rz_s.at[k - 1], self.rz_r.at[k - 1], self.p.zpeer(k))
 
-    def first(self, q):
+    def first(self, q, columns=(3, 1, 2, 0)):
         p = self.p
-        for r in (3, 1, 2, 0):
+        for r in columns:
             self.pair(r, q).wait_recv()
             at = (p.cols[r], p.zs[q], p.c)
             self.Y[at] = (self.Y[at].astype(jnp.float32) + self.PR[r, q].astype(jnp.float32)).astype(jnp.bfloat16)
@@ -354,8 +378,8 @@
 ):
     p = Place()
     bf16, f32 = jnp.bfloat16, jnp.float32
-    gather = Gather(p, X, sems[:10])
-    reduce = Reduce(p, Y, PR, RX, RH, RZ, RM, sems[10:])
+    gather = Gather(p, X, sems[:11])
+    reduce = Reduce(p, Y, PR, RX, RH, RZ, RM, sems[11:])
     tokens, model = stream_ref.shape
     rows = X.shape[-2]
     part = model // pieces
@@ -418,6 +442,8 @@
 
     gather.start()
     gather.spread_z(1)
+    outer = jnp.logical_not(p.inner)
+    pl.when(p.inner)(lambda: gather.spread_z(2))
     tile = min(512, model)
 
     y = p.s // 2
@@ -443,25 +469,27 @@
             for load in loads:
                 load.wait()
         if i == 1:
+            pl.when(outer)(lambda: gather.spread_z(2))
             gather.spread_x(1)
-            gather.spread_z(2)
+            pl.when(p.inner)(lambda: gather.spread_z(3))
+        if i == 2:
+            gather.spread_x2(0)
         if i == 3:
-            gather.spread_z(3)
+            pl.when(outer)(lambda: gather.spread_z(3))
+            gather.spread_x(2)
         if i == 4:
-            gather.spread_x2(0)
             gather.spread_x2(1)
-            gather.spread_x(2)
         if i == 5:
             gather.spread_x(3)
             own_wkv.wait()
             for k in (1, 2, 3):
                 wkv_z(k, 0).start()
         if i == 6:
-            reduce.first(1)
+            for q in (1, 0):
+                reduce.first(q, (1, 2))
         if i == 7:
             gather.spread_x2(2)
             gather.spread_x2(3)
-            reduce.second(1)
         r, b = order[i]
         gather.need(r, (2 * b, 2 * b + 1))
 
@@ -496,18 +524,20 @@
 
     lax.fori_loop(0, 8, step, 0)
     reduce.first(2)
-    reduce.third(1)
+    reduce.second(2)
     reduce.first(3)
-    reduce.second(2)
-    reduce.first(0)
+    reduce.third(2)
+    reduce.second(3)
+    reduce.first(1, (3, 0))
+    reduce.third(3)
+    reduce.first(0, (3, 0))
+    reduce.second(1)
     for k in (1, 2, 3):
         wkv_z(k, k).wait_recv()
         for d in (1, 2, 3):
             wkv_y(k, d, 0).start()
-    reduce.second(3)
-    reduce.third(2)
     reduce.second(0)
-    reduce.third(3)
+    reduce.third(1)
     reduce.third(0)
     hit_k = [ones(one) for one in named]
     fetch = slots.out_of(ones(named[0] | named[1]), hit_k)

time: 183 us -> 174 us (0.951)
  Pallas kernels: 179 us -> 170 us
    pallas_call x1, Pallas kernels: 179 us -> 170 us  [body(): pl.pallas_call(functools.partial(kernel, sections, cap, pieces), out_shap...]
where the time goes in v4:
time: 174 us
  Pallas kernels  170 us (98%)
  local copies, waits for them, and re-layouts  3.04 us (2%)
    pallas_call x1, Pallas kernels, body(): pl.pallas_call(functools.partial(kernel, sections, cap, pieces), out_shap...  170 us

profile of v4, /device:TPU:3, one launch (start us, length us, event | category | flops | bytes accessed | tf_op | source)
XLA Modules:
  0.0 173.5 jit_solution(17192863718916273753)
XLA Ops:
  0.6 169.8 %layer.1 = (bf16[16,4096]{1,0:T(8,128)(2,1)}, bf16[64,512]{1,0:T(8,128)(2,1)}) custom-call(bf16[16,4096]{1,0:T(8,128)(2,1)} %stream_ref.1, f32[1,4096]{1,0:T(1,128)} %bitcast.13, bf16[8,4096]{1,0:T(8,128)(2,1)} %bitcast.11, s32[2,16]{1,0:T(2,128)} %bitcast.15, bf16[1,448,4096]{2,1,0:T(8,128)(2,1)} %bitcast.8, bf16[1,448,4096]{2,1,0:T(8,128)(2,1)} %bitcast.9, ...), custom_call_target="tpu_custom_call" | custom-call | tf_op jit(solution)/shard_map/layer/pallas_call | solution.py:655
  170.5 1.6 copy.13
  172.0 1.5 copy.14

commit v5 on v4

--- a/solution.py
+++ b/solution.py
@@ -48,7 +48,7 @@
 
 
 def far_of(model):
-    return model // 4
+    return model // 32 * 6
 
 
 def half_of(way, half, mid):
@@ -461,68 +461,65 @@
     def wkv_y(k, d, of):
         return wkv_copy(p.zs[k], (y + of) % 4, wy_s.at[k - 1, d - 1], wy_r.at[k - 1, d - 1], section(2 * d))
 
-    order = ((0, 0), (1, 0), (2, 0), (0, 1), (3, 0), (1, 1), (2, 1), (3, 1))
+    order = (((0, 0), (1, 0)), ((2, 0), (0, 1)), ((3, 0), (1, 1)), ((2, 1), (3, 1)))
 
     def before(i):
         if i == 0:
             gather.spread_x(0)
             for load in loads:
                 load.wait()
-        if i == 1:
             pl.when(outer)(lambda: gather.spread_z(2))
             gather.spread_x(1)
             pl.when(p.inner)(lambda: gather.spread_z(3))
-        if i == 2:
+        if i == 1:
             gather.spread_x2(0)
-        if i == 3:
             pl.when(outer)(lambda: gather.spread_z(3))
             gather.spread_x(2)
-        if i == 4:
+        if i == 2:
             gather.spread_x2(1)
-        if i == 5:
             gather.spread_x(3)
             own_wkv.wait()
             for k in (1, 2, 3):
                 wkv_z(k, 0).start()
-        if i == 6:
+        if i == 3:
+            gather.spread_x2(2)
+            gather.spread_x2(3)
             for q in (1, 0):
                 reduce.first(q, (1, 2))
-        if i == 7:
-            gather.spread_x2(2)
-            gather.spread_x2(3)
-        r, b = order[i]
-        gather.need(r, (2 * b, 2 * b + 1))
+        for r, b in order[i]:
+            gather.need(r, (2 * b, 2 * b + 1))
 
     def behind(i):
-        r, b = order[i]
-        for q in (2 * b, 2 * b + 1):
-            reduce.pair(r, q).start()
+        for n in (0, 1):
+            for r, b in reversed(order[i]):
+                reduce.pair(r, 2 * b + n).start()
 
     def step(i, carry):
-        for n in range(8):
+        for n in range(4):
             pl.when(i == n)(functools.partial(before, n))
-        r = (i == 1) * 1 + (i == 2) * 2 + (i == 4) * 3 + (i == 5) * 1 + (i == 6) * 2 + (i == 7) * 3
-        b = (i == 3) * 1 + (i >= 5) * 1
-        shift = (r == 1) * 3 + (r == 2) * 1 + (r == 3) * 2
-        col = (p.x + shift) % NX
-        pair = (p.z // 2 + b) % 2
-        zs = pl.ds(2 * pair, 2)
-        value = X[col, zs].reshape(4 * rows, model)
+        halves = []
+        for n in (0, 1):
+            shift = sum((i == k) * (0, 3, 1, 2)[order[k][n][0]] for k in range(4))
+            far_pair = sum((i == k) * order[k][n][1] for k in range(4))
+            halves.append(((p.x + shift) % NX, pl.ds(2 * ((p.z // 2 + far_pair) % 2), 2)))
+        value = jnp.concatenate([X[col, zs].reshape(4 * rows, model) for col, zs in halves], axis=0)
         gate = dot_t(value, WG[...])
         up = dot_t(value, WU[...])
         H[...] = (gate / (1.0 + jnp.exp(-gate)) * up).astype(bf16)
 
         def down(n, carry):
             at = pl.ds(pl.multiple_of(n * tile, tile), tile)
-            Y[col, zs, :, :, at] = dot(H[...], WD[:, at]).astype(bf16).reshape(2, 2, rows, tile)
+            part = dot(H[...], WD[:, at]).astype(bf16)
+            for k, (col, zs) in enumerate(halves):
+                Y[col, zs, :, :, at] = part[k * 4 * rows:(k + 1) * 4 * rows].reshape(2, 2, rows, tile)
             return carry
 
         lax.fori_loop(0, model // tile, down, 0)
-        for n in range(8):
+        for n in range(4):
             pl.when(i == n)(functools.partial(behind, n))
         return carry
 
-    lax.fori_loop(0, 8, step, 0)
+    lax.fori_loop(0, 4, step, 0)
     reduce.first(2)
     reduce.second(2)
     reduce.first(3)
@@ -532,6 +529,8 @@
     reduce.third(3)
     reduce.first(0, (3, 0))
     reduce.second(1)
+    backward = slots.order(True)
+    fetch = slots.out_of(ones(named[0] | named[1]), [ones(one) for one in named])
     for k in (1, 2, 3):
         wkv_z(k, k).wait_recv()
         for d in (1, 2, 3):
@@ -539,12 +538,10 @@
     reduce.second(0)
     reduce.third(1)
     reduce.third(0)
-    hit_k = [ones(one) for one in named]
-    fetch = slots.out_of(ones(named[0] | named[1]), hit_k)
     sums = reduce.total().astype(bf16)
     for d in far:
         give(S, A, d, d_s, d_r).wait_send()
-    packed = dot(slots.order(True), jnp.concatenate([sums[:, c] for c in cut], axis=0)).astype(bf16)
+    packed = dot(backward, jnp.concatenate([sums[:, c] for c in cut], axis=0)).astype(bf16)
     S[...] = packed.reshape(S.shape)
     for d in far:
         give(S, R, d, b_s, b_r).start()
@@ -666,7 +663,7 @@
             pltpu.VMEM((hidden, model), bf16),
             pltpu.VMEM((hidden, model), bf16),
             pltpu.VMEM((hidden, model), bf16),
-            pltpu.VMEM((4 * rows, hidden), bf16),
+            pltpu.VMEM((8 * rows, hidden), bf16),
             pltpu.VMEM((4, 4, rows, model), bf16),
             pltpu.VMEM((2, 4, rows, model), bf16),
             pltpu.VMEM((4, rows, model), bf16),

time: 174 us -> 171 us (0.983)
  Pallas kernels: 170 us -> 168 us
    pallas_call x1, Pallas kernels: 170 us -> 168 us  [body(): pl.pallas_call(functools.partial(kernel, sections, cap, pieces), out_shap...]
where the time goes in v5:
time: 171 us
  Pallas kernels  168 us (98%)
  local copies, waits for them, and re-layouts  3.04 us (2%)
    pallas_call x1, Pallas kernels, body(): pl.pallas_call(functools.partial(kernel, sections, cap, pieces), out_shap...  168 us

profile of v5, /device:TPU:3, one launch (start us, length us, event | category | flops | bytes accessed | tf_op | source)
XLA Modules:
  0.0 171.3 jit_solution(17066207589628741492)
XLA Ops:
  0.6 167.6 %layer.1 = (bf16[16,4096]{1,0:T(8,128)(2,1)}, bf16[64,512]{1,0:T(8,128)(2,1)}) custom-call(bf16[16,4096]{1,0:T(8,128)(2,1)} %stream_ref.1, f32[1,4096]{1,0:T(1,128)} %bitcast.13, bf16[8,4096]{1,0:T(8,128)(2,1)} %bitcast.11, s32[2,16]{1,0:T(2,128)} %bitcast.15, bf16[1,448,4096]{2,1,0:T(8,128)(2,1)} %bitcast.8, bf16[1,448,4096]{2,1,0:T(8,128)(2,1)} %bitcast.9, ...), custom_call_target="tpu_custom_call" | custom-call | tf_op jit(solution)/shard_map/layer/pallas_call | solution.py:652
  168.2 1.6 copy.13
  169.8 1.5 copy.14
